TPU v7x, 32 devices: a whole 2x2x4 slice. The times are simulated.
32 devices in a mesh: seq: 4 (over y, x), fsdp: 8 (over z, core).
Axes of the slice: x: 2, y: 2, z: 4, core: 2. Of those that a mesh axis runs over, the one named last changes fastest.
Arguments:
- tokens: bfloat16 [8, 512, 8192], P('fsdp', 'seq'), may hold values from -6 to 6
- norm_gain: float32 [8192], replicated, may hold values from 0.3 to 3
- w_query: bfloat16 [8192, 4096], P(('seq', 'fsdp')), may hold values from -1 to 1
- key_weight: bfloat16 [8192, 512], P(('seq', 'fsdp')), may hold values from -1 to 1
- value_weight: bfloat16 [8192, 512], P(('seq', 'fsdp')), may hold values from -0.0625 to 0.0625
- w_out: bfloat16 [4096, 8192], P(None, ('seq', 'fsdp')), may hold values from -0.09375 to 0.09375
Outputs:
- result: float32 [8, 512, 8192], P('fsdp', 'seq')
All inputs are finite; a program needn't handle non-finite values.
Results may differ from a plain program's by a relative error of at most 0.04.
Values may be sent and summed in bfloat16 or wider, within the bound.
A program may use at most 128 MiB of HBM per device.

v0:
```python
import functools

import jax
import jax.numpy as jnp
from jax import lax
from jax.experimental import pallas as pl
from jax.experimental.pallas import tpu as pltpu
from jax.sharding import PartitionSpec as P

HEAD = 128
CORES = 2
PAIR = 2
SLOTS = 3
PIECES = 8
FILL = 1
MESH = pl.DeviceIdType.MESH
F32, BF16 = jnp.float32, jnp.bfloat16


class Plan:
    def __init__(self, group, devices, tokens, w_query, key_weight, w_out):
        self.group, self.devices = group, devices
        self.stops = devices // CORES
        self.fold = self.stops == 4
        self.turns = 2 if self.fold else 1
        self.count, self.features = tokens.shape
        self.width = self.features // group
        self.depth = self.width // devices
        self.length = self.count * group
        self.rows_out, self.cols_out = w_out.shape
        heads = w_query.shape[1] // HEAD
        self.group_heads = heads // (key_weight.shape[1] // HEAD)
        self.local_heads = heads // group
        self.local_width = self.local_heads * HEAD
        self.chunk = PAIR * HEAD
        self.chunks = 1 + self.local_heads // PAIR
        self.flat = self.cols_out % HEAD == 0


def when(condition, action):
    if condition is True:
        action()
    else:
        pl.when(condition)(action)


def flip(index, mask):
    result, bit = index, 1
    while bit < 8:
        side = 1 - 2 * ((index // bit) % 2)
        result = result + ((mask // bit) % 2) * bit * side
        bit *= 2
    return result


def orders(turn, group):
    bits = []
    while 2 ** len(bits) < group:
        bits.append(2 ** len(bits))
    return bits[turn:] + bits[:turn]


def kernel(plan, tokens, gain, wq, wk, wv, wo, out, gathered,
           tok, gw, nrm, part, recv, fin, ret, heads, nv, br,
           w_rx, w_in, w_out, w_sib, w_loc, n_rx, n_in, n_out, n_sib,
           x_rx, x_tx, x_loc, g_rx, g_tx, r_rx, r_tx, ret_rx, ret_tx,
           h_rx, h_tx, b_rx, b_tx, b_loc, nv_sem):
    G, S, C = plan.group, plan.stops, plan.chunks
    cw, depth, width, count = plan.chunk, plan.depth, plan.width, plan.count
    length, lw, fold, turns = plan.length, plan.local_width, plan.fold, plan.turns
    seq = lax.axis_index("seq")
    fsdp = lax.axis_index("fsdp")
    stop, core = fsdp // CORES, fsdp % CORES
    half = stop // (S // 2)
    toward = 1 - 2 * half
    far = half * (S - 1) + toward * stop
    inward = (seq, (stop + toward) * CORES + core)
    outward = (seq, (stop - toward) * CORES + core)
    sibling = (seq, stop * CORES + 1 - core)
    host = far >= 1 if fold else True
    pending = []

    def remote(source, target, send, receive, device):
        return pltpu.make_async_remote_copy(
            src_ref=source, dst_ref=target, send_sem=send, recv_sem=receive,
            device_id=device, device_id_type=MESH)

    def send(condition, make):
        when(condition, lambda: make().start())
        pending.append((condition, make))

    def origin(i):
        return jnp.where(far >= i, stop - i * toward, stop + (i - far) * toward)

    def rows(start, size):
        return pl.ds(pl.multiple_of(start * size, size), size)

    def block(j, o, c):
        return gw.at[j, rows(o * CORES + c, depth), :]

    def w_inward(j, o):
        b = block(j, o, core)
        return remote(b, b, w_in.at[j, o], w_rx.at[j, o, core], inward)

    def w_outward(j, o):
        b = block(j, o, core)
        return remote(b, b, w_out.at[j, o], w_rx.at[j, o, core], outward)

    def w_across(j, o):
        b = block(j, o, core)
        return remote(b, b, w_sib.at[j, o], w_rx.at[j, o, core], sibling)

    def w_arrive(i, j):
        o = origin(i)

        def take():
            b = block(j, o, core)
            remote(b, b, w_sib.at[j, o], w_rx.at[j, o, core], sibling).wait_recv()

        when(host, take)
        if i <= S // 2 - 1:
            send(far >= i, lambda: w_inward(j, o))
        if not fold:
            send((far < i) & (far >= 1), lambda: w_outward(j, o))
        send(host, lambda: w_across(j, o))

    def w_own_in(condition, j):
        send(condition, lambda: w_inward(j, stop))

    def w_other_core(j):
        def take():
            for i in range(S):
                o = stop if i == 0 else origin(i)
                b = block(j, o, 1 - core)
                remote(b, b, w_sib.at[j, o], w_rx.at[j, o, 1 - core], sibling).wait_recv()

        when(host, take)

    piece = plan.rows_out // PIECES

    def n_source(o, pc, own):
        cut = pl.ds(pc * piece, piece)
        return wo.at[cut, :] if own else gathered.at[o * CORES + core, cut, :]

    def n_target(o, c, pc):
        return gathered.at[o * CORES + c, pl.ds(pc * piece, piece), :]

    def n_copy(o, pc, own, sems, device):
        return remote(n_source(o, pc, own), n_target(o, core, pc),
                      sems.at[o, pc], n_rx.at[o, core, pc], device)

    def n_own_in(condition, pc):
        send(condition, lambda: n_copy(stop, pc, True, n_in, inward))

    def n_wait(o, c, pc):
        t = n_target(o, c, pc)
        remote(t, t, n_sib.at[o, pc], n_rx.at[o, c, pc], sibling).wait_recv()

    def n_arrive(i, pc):
        o = origin(i)
        n_wait(o, core, pc)
        if i <= S // 2 - 1:
            send(far >= i, lambda: n_copy(o, pc, False, n_in, inward))
        send((far < i) & (far >= 1), lambda: n_copy(o, pc, False, n_out, outward))
        send(True, lambda: n_copy(o, pc, False, n_sib, sibling))

    barrier = pltpu.get_barrier_semaphore()

    def greet(device):
        pl.semaphore_signal(barrier, inc=1, device_id=device, device_id_type=MESH)

    for k in range(1, G):
        greet((flip(seq, k), fsdp))
    greet(sibling)
    greet(inward)
    pl.when(far >= 1)(lambda: greet(outward))

    mine = rows(fsdp, depth)
    for j in range(C):
        for d in range(G):
            if j == 0:
                kv = pl.ds(d * plan.local_heads // plan.group_heads * HEAD, HEAD)
                for side, w in enumerate((wk, wv)):
                    spot = pl.ds(d * cw + side * HEAD, HEAD)
                    pltpu.make_async_copy(w.at[:, kv], gw.at[0, mine, spot], w_loc.at[0]).start()
            else:
                part_of = pl.ds(d * lw + (j - 1) * cw, cw)
                pltpu.make_async_copy(
                    wq.at[:, part_of], gw.at[j, mine, pl.ds(d * cw, cw)], w_loc.at[j]).start()
    load = pltpu.make_async_copy(tokens, tok, x_loc.at[0])
    load.start()

    pl.semaphore_wait(barrier, G + 1 + (far + S // 2 - 1) // (S // 2))

    for j in range(C):
        own = gw.at[j, mine, :]
        pltpu.make_async_copy(own, own, w_loc.at[j]).wait()
        if j == 0:
            w_own_in(True, 0)
        elif j == 1:
            w_own_in(host, 1)
        if not fold:
            send(far >= 1, lambda j=j: w_outward(j, stop))
        send(host, lambda j=j: w_across(j, stop))
    for pc in range(PIECES):
        send(far >= 1, lambda pc=pc: n_copy(stop, pc, True, n_out, outward))

    load.wait()

    def norm_rows(i, carry):
        r = rows(i, 16)
        x = tok[r, :].astype(F32)
        mean = jnp.mean(x * x, axis=-1, keepdims=True)
        tok[r, :] = (x * lax.rsqrt(mean + 1e-05) * gain[...]).astype(BF16)
        return carry

    lax.fori_loop(0, count // 16, norm_rows, 0)

    def x_copy(k):
        d = flip(seq, k)
        return remote(tok.at[:, rows(d, width)], nrm.at[0, rows(seq, count), :],
                      x_tx.at[k], x_rx.at[k], (d, fsdp))

    own_x = pltpu.make_async_copy(
        tok.at[:, rows(seq, width)], nrm.at[0, rows(seq, count), :], x_loc.at[1])
    own_x.start()
    for k in range(1, G):
        send(True, lambda k=k: x_copy(k))

    def x_wait(k):
        if k == 0:
            own_x.wait()
        else:
            spot = nrm.at[0, rows(flip(seq, k), count), :]
            remote(spot, spot, x_tx.at[k], x_rx.at[k], sibling).wait_recv()

    def g_copy(k):
        r = rows(flip(seq, k), count)
        return remote(nrm.at[0, r, :], nrm.at[turns - 1, r, :], g_tx.at[k], g_rx.at[k], inward)

    guest = far < 1
    if fold:
        for k in range(G):
            pl.when(guest)(lambda k=k: x_wait(k))
            send(guest, lambda k=k: g_copy(k))
        for j in range(1, C):
            w_own_in(guest, j)
        for pc in range(PIECES):
            n_own_in(guest, pc)

    def project(j, low, high):
        def step(i, carry):
            t, u = i // G, i % G
            bit = t + 1
            first = 1 - u // (G // 2)
            v = (G - 1 - u) % (G // 2)
            k = (v // bit) * (2 * bit) + first * bit + v % bit
            slot = j % SLOTS
            acc = jnp.dot(nrm[t], gw[j, :, rows(flip(seq, k), cw)], preferred_element_type=F32)
            part[slot, t, k] = acc.astype(BF16)

            @pl.when(first == 1)
            def _():
                remote(part.at[slot, t, k], recv.at[j, t, v], r_tx.at[j, t, k],
                       r_rx.at[j, t, v], (flip(seq, bit), fsdp)).start()

            return carry

        lax.fori_loop(low * G, high * G, step, 0)

    def alive(t, q):
        bits = orders(t, G)[:q]
        return [k for k in range(G) if not any(k & b for b in bits)]

    def landing(t, q, k):
        return sum(len(alive(t, p + 1)) for p in range(q)) + alive(t, q + 1).index(k)

    stages = len(orders(0, G))

    def r_wait(j, t, q, k):
        n = landing(t, q, k)
        spot = recv.at[j, t, n]
        remote(spot, spot, r_tx.at[j, t, 1], r_rx.at[j, t, n], sibling).wait_recv()

    def total(j, t, upto, k, store):
        tile = 64

        def step(i, carry):
            r = rows(i, tile)
            value = part[j % SLOTS, t, k, r, :].astype(F32)
            for q in range(upto):
                value = value + recv[j, t, landing(t, q, k), r, :].astype(F32)
            store(r, value.astype(BF16))
            return carry

        lax.fori_loop(0, length // tile, step, 0)

    def stage(j, q):
        for t in range(turns):
            bit = orders(t, G)[q]
            for k in alive(t, q):
                r_wait(j, t, q - 1, k)
            for k in reversed(alive(t, q)):
                if k & bit:
                    def put(r, value, t=t, k=k):
                        part[j % SLOTS, t, k, r, :] = value

                    total(j, t, q, k, put)
                    n = landing(t, q, k ^ bit)
                    remote(part.at[j % SLOTS, t, k], recv.at[j, t, n], r_tx.at[j, t, k],
                           r_rx.at[j, t, n], (flip(seq, bit), fsdp)).start()

    def ret_copy(j):
        return remote(ret.at[j], fin.at[j], ret_tx.at[j], ret_rx.at[j], outward)

    def settle(j):
        def take():
            for t in reversed(range(turns)):
                r_wait(j, t, stages - 1, 0)

                def put(r, value, t=t):
                    if t:
                        ret[j, r, :] = value
                    else:
                        fin[j, r, :] = value

                total(j, t, stages, 0, put)
                if t:
                    ret_copy(j).start()

        when(host, take)
        if fold:
            pending.append((host, lambda: ret_copy(j)))
            pl.when(guest)(lambda: remote(fin.at[j], fin.at[j], ret_tx.at[j], ret_rx.at[j],
                                          sibling).wait_recv())

    def h_copy(j, k):
        spot = heads.at[:, rows(seq * (C - 1) + j - 1, cw)]
        return remote(spot, spot, h_tx.at[j, k], h_rx.at[j, k], (flip(seq, k), fsdp))

    def attend(j):
        tile = 256

        def one_head(h, carry):
            column = rows(h, HEAD)
            for i in range(length // tile):
                seen = (i + 1) * tile
                q = fin[j, pl.ds(i * tile, tile), column]
                scores = lax.dot_general(
                    q, fin[0, pl.ds(0, seen), pl.ds(0, HEAD)],
                    (((1,), (1,)), ((), ())), preferred_element_type=F32) * (HEAD ** -0.5)
                row = lax.broadcasted_iota(jnp.int32, (tile, seen), 0) + i * tile
                col = lax.broadcasted_iota(jnp.int32, (tile, seen), 1)
                scores = jnp.where(row >= col, scores, F32(-1e30))
                top = jnp.max(scores, axis=-1, keepdims=True)
                weights = jnp.exp(scores - top)
                probs = weights * (1.0 / jnp.sum(weights, axis=-1, keepdims=True))
                mixed = jnp.dot(probs.astype(BF16), fin[0, pl.ds(0, seen), pl.ds(HEAD, HEAD)],
                                preferred_element_type=F32)
                spot = rows((seq * (C - 1) + j - 1) * PAIR + h, HEAD)
                heads[pl.ds(i * tile, tile), spot] = mixed.astype(BF16)
            return carry

        lax.fori_loop(0, PAIR, one_head, 0)
        for k in range(1, G):
            send(True, lambda k=k: h_copy(j, k))

    def target(c):
        b = seq * plan.devices + c
        return out.at[:, rows(b, plan.cols_out)] if plan.flat else out.at[b]

    def branch(o, own):
        for n in range(CORES):
            b = o * CORES + (core if n == 0 else 1 - core)
            source = wo if own and n == 0 else gathered.at[b]
            pltpu.make_async_copy(source, nv.at[n], nv_sem.at[n]).start()
        tile = 256
        for n in range(CORES):
            b = o * CORES + (core if n == 0 else 1 - core)
            pltpu.make_async_copy(wo, nv.at[n], nv_sem.at[n]).wait()

            def step(i, carry):
                r = rows(i, tile)
                acc = jnp.dot(heads[r, :], nv[n], preferred_element_type=F32)
                br[b, r, :] = acc.astype(BF16)
                return carry

            lax.fori_loop(0, length // tile, step, 0)
            for k in range(1, G):
                d = flip(seq, k)
                remote(br.at[b, rows(d, count), :], target(b), b_tx.at[k], b_rx.at[k],
                       (d, fsdp)).start()
            pltpu.make_async_copy(br.at[b, rows(seq, count), :], target(b), b_loc.at[0]).start()

    def host_first():
        for k in range(G):
            x_wait(k)
        project(0, 0, 1)
        if fold:
            for k in range(G):
                r = nrm.at[1, rows(flip(seq, k), count), :]
                remote(r, r, g_tx.at[k], g_rx.at[k], sibling).wait_recv()
            project(0, 1, 2)

    ahead = 0

    def prefetch(last):
        nonlocal ahead
        while ahead <= min(last, C - 1):
            w_arrive(1, ahead)
            ahead += 1

    prefetch(0)
    for j in range(2, C):
        w_own_in(host, j)
    for pc in range(FILL):
        n_own_in(host, pc)
    for i in range(2, S):
        w_arrive(i, 0)
    for pc in range(PIECES):
        send(True, lambda pc=pc: n_copy(stop, pc, True, n_sib, sibling))
    w_other_core(0)
    when(host, host_first)
    prefetch(1)
    filled = False
    for j in range(1, C):
        for i in range(2, S - 1):
            w_arrive(i, j)
        prefetch(j + 1)
        if S > 2:
            w_arrive(S - 1, j)
        prefetch(j + 2)
        if ahead == C and not filled:
            filled = True
            for pc in range(FILL, PIECES):
                n_own_in(host, pc)
        w_other_core(j)

        def middle(j=j):
            if j >= SLOTS:
                for t in range(turns):
                    for k in range(1, G):
                        p = part.at[j % SLOTS, t, k]
                        remote(p, p, r_tx.at[j - SLOTS, t, k], r_rx.at[j, t, 0], sibling).wait_send()
            project(j, 0, turns)
            for q in range(1, stages):
                stage(j - 1, q)

        when(host, middle)
        if j >= 2:
            settle(j - 2)
            if j >= 3:
                attend(j - 2)

    arrivals = [(i, pc) for i in range(1, S) for pc in range(PIECES)]
    taken = []

    def polls(wanted):
        for i, pc in wanted:
            if (i, pc) not in taken and i < S:
                taken.append((i, pc))
                n_arrive(i, pc)

    quarter = PIECES // 4
    polls([(1, pc) for pc in range(2 * quarter)])

    def last_stages():
        for q in range(1, stages):
            stage(C - 1, q)

    when(host, last_stages)
    polls([(2, pc) for pc in range(2 * quarter)])
    if C >= 2:
        settle(C - 2)
        if C >= 3:
            attend(C - 2)
    polls([(1, pc) for pc in range(PIECES)])
    polls([(2, pc) for pc in range(3 * quarter)])
    settle(C - 1)
    attend(C - 1)
    polls([(2, pc) for pc in range(PIECES)])
    polls([(3, pc) for pc in range(quarter)])
    for j in range(1, C):
        for k in range(1, G):
            spot = heads.at[:, rows(flip(seq, k) * (C - 1) + j - 1, cw)]
            remote(spot, spot, h_tx.at[j, k], h_rx.at[j, k], sibling).wait_recv()
    for pc in range(PIECES):
        n_wait(stop, 1 - core, pc)
    branch(stop, True)
    for i in range(1, S):
        polls([(i, pc) for pc in range(PIECES)])
        for pc in range(PIECES):
            n_wait(origin(i), 1 - core, pc)
        branch(origin(i), False)

    def all_of(side):
        span = plan.devices * plan.cols_out
        return out.at[:, rows(side, span)] if plan.flat else out.at[rows(side, plan.devices)]

    for k in range(1, G):
        remote(all_of(seq), all_of(flip(seq, k)), b_tx.at[k], b_rx.at[k], sibling).wait()
    pltpu.make_async_copy(all_of(seq), all_of(seq), b_loc.at[0]).wait()
    for condition, make in pending:
        when(condition, lambda make=make: make().wait_send())

    def drain():
        for j in range(max(0, C - SLOTS), C):
            for t in range(turns):
                for k in range(1, G):
                    p = part.at[j % SLOTS, t, k]
                    remote(p, p, r_tx.at[j, t, k], r_rx.at[j, t, 0], sibling).wait_send()

    when(host, drain)


def body(tokens, norm_gain, w_query, key_weight, value_weight, w_out):
    group, devices = lax.axis_size("seq"), lax.axis_size("fsdp")
    plan = Plan(group, devices, tokens[0], w_query, key_weight, w_out)
    G, S, C, T = plan.group, plan.stops, plan.chunks, plan.turns
    length, cw = plan.length, plan.chunk
    any_space = pl.BlockSpec(memory_space=pl.ANY)
    dma = pltpu.SemaphoreType.DMA
    if plan.flat:
        out_shape = (plan.count, plan.features)
    else:
        out_shape = (G * devices, plan.count, plan.cols_out)
    outward = (1, 1) if plan.fold else (C, S)
    branches, _ = pl.pallas_call(
        functools.partial(kernel, plan),
        out_shape=(
            jax.ShapeDtypeStruct(out_shape, BF16),
            jax.ShapeDtypeStruct((devices,) + w_out.shape, BF16),
        ),
        in_specs=[any_space, pl.BlockSpec(memory_space=pltpu.VMEM)] + [any_space] * 4,
        out_specs=(any_space, any_space),
        scratch_shapes=[
            pltpu.VMEM((plan.count, plan.features), BF16),
            pltpu.VMEM((C, plan.width, G * cw), BF16),
            pltpu.VMEM((T, length, plan.width), BF16),
            pltpu.VMEM((SLOTS, T, G, length, cw), BF16),
            pltpu.VMEM((C, T, G - 1, length, cw), BF16),
            pltpu.VMEM((C, length, cw), BF16),
            pltpu.VMEM((C if plan.fold else 1, length, cw), BF16),
            pltpu.VMEM((length, plan.rows_out), BF16),
            pltpu.VMEM((CORES,) + w_out.shape, BF16),
            pltpu.VMEM((devices, length, plan.cols_out), BF16),
            dma((C, S, CORES)), dma((C, S)), dma(outward), dma((C, S)), dma((C,)),
            dma((S, CORES, PIECES)), dma((S, PIECES)), dma((S, PIECES)), dma((S, PIECES)),
            dma((G,)), dma((G,)), dma((2,)), dma((G,)), dma((G,)),
            dma((C, T, G)), dma((C, T, G)), dma((C,)), dma((C,)),
            dma((C, G)), dma((C, G)), dma((G,)), dma((G,)), dma((1,)), dma((CORES,)),
        ],
        compiler_params=pltpu.CompilerParams(
            collective_id=0, has_side_effects=True, vmem_limit_bytes=67043328),
    )(tokens[0], norm_gain[None], w_query, key_weight, value_weight, w_out)
    if not plan.flat:
        branches = jnp.transpose(branches, (1, 0, 2)).reshape(plan.count, plan.features)
    return tokens.astype(F32) + branches[None].astype(F32)


def solution(mesh):
    placed = (
        P("fsdp", "seq", None),
        P(),
        P(("seq", "fsdp"), None),
        P(("seq", "fsdp"), None),
        P(("seq", "fsdp"), None),
        P(None, ("seq", "fsdp")),
    )
    return jax.shard_map(
        body, mesh=mesh, in_specs=placed, out_specs=P("fsdp", "seq", None), check_vma=False
    )
```

profile of v0, /device:TPU:0, one launch (start us, length us, event | category | flops | bytes accessed | tf_op | source)
XLA Modules:
  0.0 293.3 jit_solution(16160956559634864284)
XLA Ops:
  0.0 288.6 %shard_map.64 = (bf16[128,8192]{1,0:T(8,128)(2,1)}, bf16[8,4096,256]{2,1,0:T(8,128)(2,1)}) custom-call(bf16[128,8192]{1,0:T(8,128)(2,1)} %bitcast.5, f32[1,8192]{1,0:T(1,128)} %bitcast.6, bf16[256,4096]{1,0:T(8,128)(2,1)} %wq.1, bf16[256,512]{1,0:T(8,128)(2,1)} %wk.1, bf16[256,512]{1,0:T(8,128)(2,1)} %wv.1, bf16[4096,256]{1,0:T(8,128)(2,1)} %wo.1), custom_call_target="tpu_custom_call" | custom-call | tf_op jit(solution)/shard_map/pallas_call | solution.py:528
  288.6 4.8 %convert_add_fusion = f32[1,128,8192]{2,1,0:T(8,128)} fusion(bf16[1,128,8192]{2,1,0:T(8,128)(2,1)} %param.6, bf16[128,8192]{1,0:T(8,128)(2,1)} %get-tuple-element.6), kind=kLoop, calls=%fused_computation | loop fusion | flops 3145728 | bytes 8388608 | tf_op jit(solution)/shard_map/add | solution.py:558
where the time goes:
time: 294 us; the launch traced here: 293 us
  Pallas kernels  289 us (98%)
  other arithmetic  4.76 us (2%)
    pallas_call x1, Pallas kernels, body(): pl.pallas_call(functools.partial(kernel, plan), out_shape=(jax.ShapeDtype...  289 us

commit v1 on v0

v1 whole, which is shorter than its diff:
```python
import functools

import jax
import jax.numpy as jnp
from jax import lax
from jax.experimental import pallas as pl
from jax.experimental.pallas import tpu as pltpu
from jax.sharding import PartitionSpec as P

HEAD = 128
CORES = 2
PAIR = 2
SLOTS = 3
PIECES = 8
FILL = 6
MESH = pl.DeviceIdType.MESH
F32, BF16 = jnp.float32, jnp.bfloat16


class Plan:
    def __init__(self, group, devices, tokens, w_query, key_weight, w_out):
        self.group, self.devices = group, devices
        self.stops = devices // CORES
        self.fold = self.stops == 4
        self.turns = 2 if self.fold else 1
        self.count, self.features = tokens.shape
        self.width = self.features // group
        self.depth = self.width // devices
        self.length = self.count * group
        self.rows_out, self.cols_out = w_out.shape
        heads = w_query.shape[1] // HEAD
        self.group_heads = heads // (key_weight.shape[1] // HEAD)
        self.local_heads = heads // group
        self.local_width = self.local_heads * HEAD
        self.chunk = PAIR * HEAD
        self.chunks = 1 + self.local_heads // PAIR
        self.flat = self.cols_out % HEAD == 0
        self.parts = self.cols_out // HEAD if self.flat else 1
        self.part_cols = self.cols_out // self.parts
        self.part_rows = PIECES // self.parts
        self.units = 1 if self.flat else CORES


def when(condition, action):
    def run():
        action()

    if condition is True:
        run()
    else:
        pl.when(condition)(run)


def both_true(one, other):
    return other if one is True else one & other


def flip(index, mask):
    result, bit = index, 1
    while bit < 8:
        side = 1 - 2 * ((index // bit) % 2)
        result = result + ((mask // bit) % 2) * bit * side
        bit *= 2
    return result


def orders(turn, group):
    bits = []
    while 2 ** len(bits) < group:
        bits.append(2 ** len(bits))
    return bits[turn:] + bits[:turn]


def kernel(plan, tokens, gain, wq, wk, wv, wo, out, gathered,
           tok, gw, nrm, part, recv, fin, ret, heads, nv, br, br_acc,
           w_rx, w_in, w_out, w_sib, w_loc, n_rx, n_in, n_out, n_sib,
           x_rx, x_tx, x_loc, g_rx, g_tx, r_rx, r_tx, ret_rx, ret_tx,
           h_rx, h_tx, b_rx, b_tx, b_loc, nv_sem):
    G, S, C = plan.group, plan.stops, plan.chunks
    cw, depth, width, count = plan.chunk, plan.depth, plan.width, plan.count
    length, lw, fold, turns = plan.length, plan.local_width, plan.fold, plan.turns
    seq = lax.axis_index("seq")
    fsdp = lax.axis_index("fsdp")
    stop, core = fsdp // CORES, fsdp % CORES
    half = stop // (S // 2)
    toward = 1 - 2 * half
    far = half * (S - 1) + toward * stop
    inward = (seq, (stop + toward) * CORES + core)
    outward = (seq, (stop - toward) * CORES + core)
    sibling = (seq, stop * CORES + 1 - core)
    host = far >= 1 if fold else True
    pending = []

    def remote(source, target, send, receive, device):
        return pltpu.make_async_remote_copy(
            src_ref=source, dst_ref=target, send_sem=send, recv_sem=receive,
            device_id=device, device_id_type=MESH)

    def send(condition, make):
        when(condition, lambda: make().start())
        pending.append((condition, make))

    def origin(i):
        return jnp.where(far >= i, stop - i * toward, stop + (i - far) * toward)

    def rows(start, size):
        return pl.ds(pl.multiple_of(start * size, size), size)

    def block(j, o, c):
        return gw.at[j, rows(o * CORES + c, depth), :]

    def w_inward(j, o):
        b = block(j, o, core)
        return remote(b, b, w_in.at[j, o], w_rx.at[j, o, core], inward)

    def w_outward(j, o):
        b = block(j, o, core)
        return remote(b, b, w_out.at[j, o], w_rx.at[j, o, core], outward)

    def w_across(j, o):
        b = block(j, o, core)
        return remote(b, b, w_sib.at[j, o], w_rx.at[j, o, core], sibling)

    def w_arrive(i, j):
        with jax.named_scope(f"w{i}_{j}"):
            w_arrive_body(i, j)

    def w_arrive_body(i, j):
        o = origin(i)

        def take():
            b = block(j, o, core)
            remote(b, b, w_sib.at[j, o], w_rx.at[j, o, core], sibling).wait_recv()

        when(host, take)
        if i <= S // 2 - 1:
            send(far >= i, lambda: w_inward(j, o))
        if not fold:
            send((far < i) & (far >= 1), lambda: w_outward(j, o))
        send(host, lambda: w_across(j, o))

    def w_own_in(condition, j):
        send(condition, lambda: w_inward(j, stop))

    def w_other_core(j):
        with jax.named_scope(f"wsib_{j}"):
            w_other_core_body(j)

    def w_other_core_body(j):
        def take():
            for i in range(S):
                o = stop if i == 0 else origin(i)
                b = block(j, o, 1 - core)
                remote(b, b, w_sib.at[j, o], w_rx.at[j, o, 1 - core], sibling).wait_recv()

        when(host, take)

    per_part = plan.part_rows
    piece = plan.rows_out // per_part
    pw = plan.part_cols

    def n_cut(pc):
        return pl.ds(pc % per_part * piece, piece), pl.ds(pc // per_part * pw, pw)

    def n_source(o, pc, own):
        r, c = n_cut(pc)
        return wo.at[r, c] if own else gathered.at[o * CORES + core, r, c]

    def n_target(o, c, pc):
        r, cut = n_cut(pc)
        return gathered.at[o * CORES + c, r, cut]

    def n_copy(o, pc, own, sems, device):
        return remote(n_source(o, pc, own), n_target(o, core, pc),
                      sems.at[o, pc], n_rx.at[o, core, pc], device)

    def n_own_in(condition, pc):
        send(condition, lambda: n_copy(stop, pc, True, n_in, inward))

    def n_wait(o, c, pc):
        t = n_target(o, c, pc)
        remote(t, t, n_sib.at[o, pc], n_rx.at[o, c, pc], sibling).wait_recv()

    def n_arrive(i, pc, who=True):
        o = origin(i)

        def take():
            with jax.named_scope(f"n{i}_{pc}"):
                n_wait(o, core, pc)

        when(who, take)
        if i <= S // 2 - 1:
            send(both_true(who, far >= i), lambda: n_copy(o, pc, False, n_in, inward))
        send(both_true(who, (far < i) & (far >= 1)),
             lambda: n_copy(o, pc, False, n_out, outward))
        send(who, lambda: n_copy(o, pc, False, n_sib, sibling))

    barrier = pltpu.get_barrier_semaphore()

    def greet(device):
        pl.semaphore_signal(barrier, inc=1, device_id=device, device_id_type=MESH)

    for k in range(1, G):
        greet((flip(seq, k), fsdp))
    greet(sibling)
    greet(inward)
    pl.when(far >= 1)(lambda: greet(outward))

    mine = rows(fsdp, depth)
    for j in range(C):
        for d in range(G):
            if j == 0:
                kv = pl.ds(d * plan.local_heads // plan.group_heads * HEAD, HEAD)
                for side, w in enumerate((wk, wv)):
                    spot = pl.ds(d * cw + side * HEAD, HEAD)
                    pltpu.make_async_copy(w.at[:, kv], gw.at[0, mine, spot], w_loc.at[0]).start()
            else:
                part_of = pl.ds(d * lw + (j - 1) * cw, cw)
                pltpu.make_async_copy(
                    wq.at[:, part_of], gw.at[j, mine, pl.ds(d * cw, cw)], w_loc.at[j]).start()
    load = pltpu.make_async_copy(tokens, tok, x_loc.at[0])
    load.start()

    pl.semaphore_wait(barrier, G + 1 + (far + S // 2 - 1) // (S // 2))

    for j in range(C):
        own = gw.at[j, mine, :]
        pltpu.make_async_copy(own, own, w_loc.at[j]).wait()
        if j == 0:
            w_own_in(True, 0)
        elif j == 1:
            w_own_in(True, 1)
        if not fold:
            send(far >= 1, lambda j=j: w_outward(j, stop))
        send(host, lambda j=j: w_across(j, stop))
    for pc in range(PIECES):
        send(far >= 1, lambda pc=pc: n_copy(stop, pc, True, n_out, outward))

    load.wait()

    def norm_rows(i, carry):
        r = rows(i, 16)
        x = tok[r, :].astype(F32)
        mean = jnp.mean(x * x, axis=-1, keepdims=True)
        tok[r, :] = (x * lax.rsqrt(mean + 1e-05) * gain[...]).astype(BF16)
        return carry

    lax.fori_loop(0, count // 16, norm_rows, 0)

    def x_copy(k):
        d = flip(seq, k)
        return remote(tok.at[:, rows(d, width)], nrm.at[0, rows(seq, count), :],
                      x_tx.at[k], x_rx.at[k], (d, fsdp))

    own_x = pltpu.make_async_copy(
        tok.at[:, rows(seq, width)], nrm.at[0, rows(seq, count), :], x_loc.at[1])
    own_x.start()
    for k in range(1, G):
        send(True, lambda k=k: x_copy(k))

    def x_wait(k):
        if k == 0:
            own_x.wait()
        else:
            spot = nrm.at[0, rows(flip(seq, k), count), :]
            remote(spot, spot, x_tx.at[k], x_rx.at[k], sibling).wait_recv()

    def g_copy(k):
        r = rows(flip(seq, k), count)
        return remote(nrm.at[0, r, :], nrm.at[turns - 1, r, :], g_tx.at[k], g_rx.at[k], inward)

    guest = far < 1
    if fold:
        for k in range(G):
            pl.when(guest)(lambda k=k: x_wait(k))
            send(guest, lambda k=k: g_copy(k))
        for j in range(2, C):
            w_own_in(guest, j)
        for pc in range(PIECES):
            n_own_in(guest, pc)

    def project(j, low, high):
        with jax.named_scope(f"project_{j}"):
            project_body(j, low, high)

    def project_body(j, low, high):
        def step(i, carry):
            t, k = i // G, G - 1 - i % G
            slot = j % SLOTS
            acc = jnp.dot(nrm[t], gw[j, :, rows(flip(seq, k), cw)], preferred_element_type=F32)
            for u in range(PAIR):
                part[slot, t, u, k] = acc[:, u * HEAD:(u + 1) * HEAD].astype(BF16)
            for u in range(PAIR):
                bit = u + 1

                @pl.when((k // bit) % 2 == 1)
                def _(u=u, bit=bit):
                    n = (k // (2 * bit)) * bit + k % bit
                    remote(part.at[slot, t, u, k], recv.at[j, t, u, n], r_tx.at[j, t, u, k],
                           r_rx.at[j, t, u, n], (flip(seq, bit), fsdp)).start()

            return carry

        lax.fori_loop(low * G, high * G, step, 0)

    def alive(u, q):
        bits = orders(u, G)[:q]
        return [k for k in range(G) if not any(k & b for b in bits)]

    def landing(u, q, k):
        return sum(len(alive(u, p + 1)) for p in range(q)) + alive(u, q + 1).index(k)

    stages = len(orders(0, G))

    def r_wait(j, t, u, q, k):
        n = landing(u, q, k)
        spot = recv.at[j, t, u, n]
        remote(spot, spot, r_tx.at[j, t, u, 1], r_rx.at[j, t, u, n], sibling).wait_recv()

    def total(j, t, u, upto, k, store):
        tile = 128
        for q in range(upto):
            r_wait(j, t, u, q, k)

        def step(i, carry):
            r = rows(i, tile)
            value = part[j % SLOTS, t, u, k, r, :].astype(F32)
            for q in range(upto):
                value = value + recv[j, t, u, landing(u, q, k), r, :].astype(F32)
            store(r, value.astype(BF16))
            return carry

        lax.fori_loop(0, length // tile, step, 0)

    def stage(j, t):
        with jax.named_scope(f"stage_{j}_{t}"):
            stage_body(j, t)

    def stage_body(j, t):
        for q in range(1, stages):
            for u in range(PAIR):
                bit = orders(u, G)[q]
                for k in reversed(alive(u, q)):
                    if k & bit:
                        def put(r, value, u=u, k=k):
                            part[j % SLOTS, t, u, k, r, :] = value

                        total(j, t, u, q, k, put)
                        n = landing(u, q, k ^ bit)
                        remote(part.at[j % SLOTS, t, u, k], recv.at[j, t, u, n],
                               r_tx.at[j, t, u, k], r_rx.at[j, t, u, n],
                               (flip(seq, bit), fsdp)).start()

    def ret_copy(j):
        return remote(ret.at[j], fin.at[j], ret_tx.at[j], ret_rx.at[j], outward)

    def settle(j, t):
        with jax.named_scope(f"settle_{j}_{t}"):
            settle_body(j, t)

    def settle_body(j, t):
        for u in range(PAIR):
            def put(r, value, u=u):
                if t:
                    ret[j, r, pl.ds(u * HEAD, HEAD)] = value
                else:
                    fin[j, r, pl.ds(u * HEAD, HEAD)] = value

            total(j, t, u, stages, 0, put)
        if t:
            ret_copy(j).start()

    def returned(j):
        if fold:
            pending.append((host, lambda: ret_copy(j)))

            @pl.when(guest)
            def _():
                with jax.named_scope(f"returned_{j}"):
                    remote(fin.at[j], fin.at[j], ret_tx.at[j], ret_rx.at[j], sibling).wait_recv()

    def sent(j):
        for t in range(turns):
            for u in range(PAIR):
                for k in range(1, G):
                    p = part.at[j % SLOTS, t, u, k]
                    remote(p, p, r_tx.at[j, t, u, k], r_rx.at[j, t, u, 0], sibling).wait_send()

    relayed = G == 4
    near = [1, 2] if relayed else list(range(1, G))

    def h_spot(owner, j):
        return heads.at[:, rows(owner * (C - 1) + j - 1, cw)]

    def h_half(owner, j, u):
        return heads.at[:, rows((owner * (C - 1) + j - 1) * PAIR + u, HEAD)]

    def h_copy(j, k):
        spot = h_spot(seq, j)
        return remote(spot, spot, h_tx.at[j, k], h_rx.at[j, k], (flip(seq, k), fsdp))

    def h_relay(j, u):
        came, goes = orders(u, G)[:2]
        half = h_half(flip(seq, came), j, u)
        return remote(half, half, h_tx.at[j, G + u], h_rx.at[j, G + u], (flip(seq, goes), fsdp))

    def h_wait(j):
        with jax.named_scope(f"hwait_{j}"):
            for k in near:
                spot = h_spot(flip(seq, k), j)
                remote(spot, spot, h_tx.at[j, k], h_rx.at[j, k], sibling).wait_recv()

    def relay(j):
        h_wait(j)
        if relayed:
            for u in range(PAIR):
                send(True, lambda u=u: h_relay(j, u))

    def h_last(j):
        if relayed:
            with jax.named_scope(f"hlast_{j}"):
                for u in range(PAIR):
                    half = h_half(flip(seq, G - 1), j, u)
                    remote(half, half, h_tx.at[j, G + u], h_rx.at[j, G + u], sibling).wait_recv()

    def attend(j, condition=True):
        when(condition, lambda: mix(j))
        for k in near:
            pending.append((condition, lambda k=k: h_copy(j, k)))

    def mix(j):
        with jax.named_scope(f"attend_{j}"):
            mix_body(j)

    def mix_body(j):
        tile = 256

        def one_head(h, carry):
            column = rows(h, HEAD)
            for i in range(length // tile):
                seen = (i + 1) * tile
                q = fin[j, pl.ds(i * tile, tile), column]
                scores = lax.dot_general(
                    q, fin[0, pl.ds(0, seen), pl.ds(0, HEAD)],
                    (((1,), (1,)), ((), ())), preferred_element_type=F32) * (HEAD ** -0.5)
                row = lax.broadcasted_iota(jnp.int32, (tile, seen), 0) + i * tile
                col = lax.broadcasted_iota(jnp.int32, (tile, seen), 1)
                scores = jnp.where(row >= col, scores, F32(-1e30))
                top = jnp.max(scores, axis=-1, keepdims=True)
                weights = jnp.exp(scores - top)
                probs = weights * (1.0 / jnp.sum(weights, axis=-1, keepdims=True))
                mixed = jnp.dot(probs.astype(BF16), fin[0, pl.ds(0, seen), pl.ds(HEAD, HEAD)],
                                preferred_element_type=F32)
                spot = rows((seq * (C - 1) + j - 1) * PAIR + h, HEAD)
                heads[pl.ds(i * tile, tile), spot] = mixed.astype(BF16)
            return carry

        lax.fori_loop(0, PAIR, one_head, 0)
        for k in near:
            h_copy(j, k).start()

    def target(c, h):
        b = seq * plan.devices + c
        if not plan.flat:
            return out.at[b]
        return out.at[:, rows(b * plan.parts + h, pw)]

    def n_spot(h, c, r):
        if plan.flat:
            return nv.at[h, 0, r, pl.ds(c * pw, pw)]
        return nv.at[h, c, r, :]

    def n_load(o, own, h, r):
        copies = []
        for n in range(CORES):
            c = core if n == 0 else 1 - core
            cut = pl.ds(h * pw, pw)
            source = wo.at[r, cut] if own and n == 0 else gathered.at[o * CORES + c, r, cut]
            copies.append(pltpu.make_async_copy(source, n_spot(h, n, r), nv_sem.at[h, n]))
        return copies

    def br_spot(o, h, n, r):
        if plan.flat:
            return br.at[o, h, 0, r, pl.ds(n * pw, pw)]
        return br.at[o, h, n, r, :]

    def br_send(o, h):
        for n in range(CORES):
            c = core if n == 0 else 1 - core
            for k in range(1, G):
                d = flip(seq, k)
                remote(br_spot(o, h, n, rows(d, count)), target(o * CORES + c, h),
                       b_tx.at[k], b_rx.at[k], (d, fsdp)).start()
            pltpu.make_async_copy(br_spot(o, h, n, rows(seq, count)), target(o * CORES + c, h),
                                  b_loc.at[0]).start()

    tile = 256
    whole = pl.ds(0, plan.rows_out)

    def branch(o, own):
        with jax.named_scope("branch"):
            branch_body(o, own)

    def branch_body(o, own):
        copies = [n_load(o, own, h, whole) for h in range(plan.parts)]
        for pair in copies:
            for copy in pair:
                copy.start()
        for h in range(plan.parts):
            for copy in copies[h]:
                copy.wait()
            for unit in range(plan.units):
                def step(i, carry, h=h, unit=unit):
                    r = rows(i, tile)
                    acc = jnp.dot(heads[r, :], nv[h, unit], preferred_element_type=F32)
                    br[o, h, unit, r, :] = acc.astype(BF16)
                    return carry

                lax.fori_loop(0, length // tile, step, 0)
            br_send(o, h)

    def branch_last(i):
        o = origin(i)
        for pc in range(PIECES):
            polls(i, pc, pc + 2)
            with jax.named_scope(f"nsib_{i}_{pc}"):
                n_wait(o, 1 - core, pc)
            h, q = pc // per_part, pc % per_part
            copies = n_load(o, False, h, pl.ds(q * piece, piece))
            for copy in copies:
                copy.start()
            for copy in copies:
                copy.wait()
            for unit in range(plan.units):
                def step(i, carry, h=h, q=q, unit=unit):
                    r = rows(i, tile)
                    cut = pl.ds(q * piece, piece)
                    acc = jnp.dot(heads[r, cut], nv[h, unit, cut, :], preferred_element_type=F32)
                    if q:
                        acc = acc + br_acc[unit, r, :]
                    if q < per_part - 1:
                        br_acc[unit, r, :] = acc
                    else:
                        br[o, h, unit, r, :] = acc.astype(BF16)
                    return carry

                lax.fori_loop(0, length // tile, step, 0)
            if q == per_part - 1:
                br_send(o, h)

    def both(action):
        for t in range(turns):
            action(t)

    early = min(2, C)

    def both_early(action):
        for j in range(early):
            action(j, 1)

    def take_chunk(j):
        for i in range(2, S):
            w_arrive(i, j)
        w_other_core(j)

    for j in range(early):
        w_arrive(1, j)
    for pc in range(FILL):
        n_own_in(host, pc)
    if early < C:
        w_own_in(host, early)
    for j in range(early):
        take_chunk(j)
        if j == 0:
            when(host, lambda: [x_wait(k) for k in range(G)])
        when(host, lambda j=j: project(j, 0, 1))
        if j == 0:
            for pc in range(PIECES):
                send(True, lambda pc=pc: n_copy(stop, pc, True, n_sib, sibling))

    def own_early():
        for j in range(early):
            stage(j, 0)
        for j in range(early):
            settle(j, 0)
        for j in range(1, early):
            mix(j)

    def guests_early():
        with jax.named_scope("gwait"):
            for k in range(G):
                r = nrm.at[1, rows(flip(seq, k), count), :]
                remote(r, r, g_tx.at[k], g_rx.at[k], sibling).wait_recv()
        for j in range(early):
            project(j, 1, 2)

    when(host, own_early)
    for j in range(1, early):
        for k in near:
            pending.append((host, lambda j=j, k=k: h_copy(j, k)))
    taken = []
    relays = [j for j in range(1, C)]

    def polls(i, first, last, role=None):
        for pc in range(first * PIECES // 8, min(last, 8) * PIECES // 8):
            for who, name in ((host, "host"), (guest, "guest")):
                if (i, pc, name) in taken or i >= S or role not in (None, name):
                    continue
                if name == "host" and role is None and (i, pc, "guest") not in taken:
                    taken.extend([(i, pc, "host"), (i, pc, "guest")])
                    n_arrive(i, pc)
                elif name == "host" or fold:
                    taken.append((i, pc, name))
                    n_arrive(i, pc, who)

    def gather(i):
        polls(i, 0, 8)
        with jax.named_scope(f"nsib_{i}"):
            for pc in range(PIECES):
                n_wait(origin(i), 1 - core, pc)

    def relay_to(j):
        while relays and relays[0] <= j:
            relay(relays.pop(0))

    def close(j):
        when(host, lambda: both(lambda t: settle(j, t)))
        returned(j)

    def forward(j):
        if early <= j < C:
            w_arrive(1, j)
            if j + 1 < C:
                w_own_in(host, j + 1)

    polls(2, 0, 2, "host")
    if fold:
        when(host, guests_early)
    polls(2, 2, 5, "host")
    forward(early)
    if fold:
        when(host, lambda: both_early(stage))
    polls(2, 5, FILL, "host")
    if fold:
        when(host, lambda: both_early(settle))
    for j in range(early + 1, C):
        forward(j)
    for pc in range(FILL, PIECES):
        n_own_in(host, pc)
    if fold:
        polls(1, 0, 8, "guest")
        polls(2, 0, FILL, "guest")
        for e in range(early):
            returned(e)
        for e in range(1, early):
            attend(e, guest)
    waiting = None
    for j in range(early, C):
        take_chunk(j)
        if j >= SLOTS:
            when(host, lambda j=j: sent(j - SLOTS))
        when(host, lambda j=j: project(j, 0, turns))
        if j == C - 1:
            polls(1, 6, 8, "host")
            polls(2, 6, 7, "host")
        if waiting is not None:
            close(waiting)
        relay_to(j - 2)
        when(host, lambda j=j: both(lambda t: stage(j, t)))
        if j == C - 1:
            polls(2, 7, 8, "host")
        if waiting is not None:
            attend(waiting)
        waiting = j
        if j < C - 2:
            close(j)
            attend(j)
            waiting = None
        if j == C - 2:
            polls(1, 0, 6, "host")
    polls(3, 0, 1, "host")
    polls(2, 0, 8, "guest")
    if waiting is not None:
        close(waiting)
        attend(waiting)
    polls(3, 1, 2, "host")
    relay_to(C - 2)
    polls(3, 2, 3, "host")
    relay_to(C - 1)
    polls(3, 3, 4, "host")
    polls(3, 0, 2, "guest")
    for j in range(1, C):
        h_last(j)
    for pc in range(PIECES):
        n_wait(stop, 1 - core, pc)
    branch(stop, True)
    polls(3, 4, 5, "host")
    polls(3, 2, 3, "guest")
    for i in range(1, S - 1):
        gather(i)
        branch(origin(i), False)
        polls(3, 4 + i, 5 + i, "host")
        polls(3, 2 + i, 3 + i, "guest")
    polls(3, 0, 8, "host")
    if S > 1:
        branch_last(S - 1)

    def all_of(side):
        span = plan.devices * plan.cols_out
        return out.at[:, rows(side, span)] if plan.flat else out.at[rows(side, plan.devices)]

    with jax.named_scope("sends"):
        for condition, make in pending:
            when(condition, lambda make=make: make().wait_send())
        when(host, lambda: [sent(j) for j in range(max(0, C - SLOTS), C)])
    with jax.named_scope("bwait"):
        for k in range(1, G):
            remote(all_of(seq), all_of(flip(seq, k)), b_tx.at[k], b_rx.at[k], sibling).wait()
        pltpu.make_async_copy(all_of(seq), all_of(seq), b_loc.at[0]).wait()


def body(tokens, norm_gain, w_query, key_weight, value_weight, w_out):
    group, devices = lax.axis_size("seq"), lax.axis_size("fsdp")
    plan = Plan(group, devices, tokens[0], w_query, key_weight, w_out)
    G, S, C, T = plan.group, plan.stops, plan.chunks, plan.turns
    length, cw = plan.length, plan.chunk
    unit_cols = plan.part_cols * CORES // plan.units
    any_space = pl.BlockSpec(memory_space=pl.ANY)
    dma = pltpu.SemaphoreType.DMA
    if plan.flat:
        out_shape = (plan.count, plan.features)
    else:
        out_shape = (G * devices, plan.count, plan.cols_out)
    outward = (1, 1) if plan.fold else (C, S)
    branches, _ = pl.pallas_call(
        functools.partial(kernel, plan),
        out_shape=(
            jax.ShapeDtypeStruct(out_shape, BF16),
            jax.ShapeDtypeStruct((devices,) + w_out.shape, BF16),
        ),
        in_specs=[any_space, pl.BlockSpec(memory_space=pltpu.VMEM)] + [any_space] * 4,
        out_specs=(any_space, any_space),
        scratch_shapes=[
            pltpu.VMEM((plan.count, plan.features), BF16),
            pltpu.VMEM((C, plan.width, G * cw), BF16),
            pltpu.VMEM((T, length, plan.width), BF16),
            pltpu.VMEM((SLOTS, T, PAIR, G, length, HEAD), BF16),
            pltpu.VMEM((C, T, PAIR, G - 1, length, HEAD), BF16),
            pltpu.VMEM((C, length, cw), BF16),
            pltpu.VMEM((C if plan.fold else 1, length, cw), BF16),
            pltpu.VMEM((length, plan.rows_out), BF16),
            pltpu.VMEM((plan.parts, plan.units, plan.rows_out, unit_cols), BF16),
            pltpu.VMEM((S, plan.parts, plan.units, length, unit_cols), BF16),
            pltpu.VMEM((plan.units, length, unit_cols), F32),
            dma((C, S, CORES)), dma((C, S)), dma(outward), dma((C, S)), dma((C,)),
            dma((S, CORES, PIECES)), dma((S, PIECES)), dma((S, PIECES)), dma((S, PIECES)),
            dma((G,)), dma((G,)), dma((2,)), dma((G,)), dma((G,)),
            dma((C, T, PAIR, G)), dma((C, T, PAIR, G)), dma((C,)), dma((C,)),
            dma((C, G + PAIR)), dma((C, G + PAIR)), dma((G,)), dma((G,)), dma((1,)), dma((plan.parts, CORES)),
        ],
        compiler_params=pltpu.CompilerParams(
            collective_id=0, has_side_effects=True, vmem_limit_bytes=67043328),
    )(tokens[0], norm_gain[None], w_query, key_weight, value_weight, w_out)
    if not plan.flat:
        branches = jnp.transpose(branches, (1, 0, 2)).reshape(plan.count, plan.features)
    return tokens.astype(F32) + branches[None].astype(F32)


def solution(mesh):
    placed = (
        P("fsdp", "seq", None),
        P(),
        P(("seq", "fsdp"), None),
        P(("seq", "fsdp"), None),
        P(("seq", "fsdp"), None),
        P(None, ("seq", "fsdp")),
    )
    return jax.shard_map(
        body, mesh=mesh, in_specs=placed, out_specs=P("fsdp", "seq", None), check_vma=False
    )
```

time: 294 us -> 249 us (0.85)
  Pallas kernels: 289 us -> 244 us
    pallas_call x1, Pallas kernels: 289 us -> 244 us  [body(): pl.pallas_call(functools.partial(kernel, plan), out_shape=(jax.ShapeDtype...]
where the time goes in v1:
time: 249 us
  Pallas kernels  244 us (98%)
  other arithmetic  4.76 us (2%)
    pallas_call x1, Pallas kernels, body(): pl.pallas_call(functools.partial(kernel, plan), out_shape=(jax.ShapeDtype...  244 us

profile of v1, /device:TPU:0, one launch (start us, length us, event | category | flops | bytes accessed | tf_op | source)
XLA Modules:
  0.0 248.8 jit_solution(218320261788987086)
XLA Ops:
  0.0 244.0 %shard_map.64 = (bf16[128,8192]{1,0:T(8,128)(2,1)}, bf16[8,4096,256]{2,1,0:T(8,128)(2,1)}) custom-call(bf16[128,8192]{1,0:T(8,128)(2,1)} %bitcast.5, f32[1,8192]{1,0:T(1,128)} %bitcast.6, bf16[256,4096]{1,0:T(8,128)(2,1)} %wq.1, bf16[256,512]{1,0:T(8,128)(2,1)} %wk.1, bf16[256,512]{1,0:T(8,128)(2,1)} %wv.1, bf16[4096,256]{1,0:T(8,128)(2,1)} %wo.1), custom_call_target="tpu_custom_call" | custom-call | tf_op jit(solution)/shard_map/pallas_call | solution.py:735
  244.0 4.8 %convert_add_fusion = f32[1,128,8192]{2,1,0:T(8,128)} fusion(bf16[1,128,8192]{2,1,0:T(8,128)(2,1)} %param.6, bf16[128,8192]{1,0:T(8,128)(2,1)} %get-tuple-element.6), kind=kLoop, calls=%fused_computation | loop fusion | flops 3145728 | bytes 8388608 | tf_op jit(solution)/shard_map/add | solution.py:766

commit v2 on v1

--- a/solution.py
+++ b/solution.py
@@ -10,9 +10,9 @@
 HEAD = 128
 CORES = 2
 PAIR = 2
-SLOTS = 3
+SLOTS = 2
 PIECES = 8
-FILL = 6
+FILL = 4
 MESH = pl.DeviceIdType.MESH
 F32, BF16 = jnp.float32, jnp.bfloat16
 
@@ -39,6 +39,7 @@
         self.part_cols = self.cols_out // self.parts
         self.part_rows = PIECES // self.parts
         self.units = 1 if self.flat else CORES
+        self.kept = self.stops - 1 if self.fold else 1
 
 
 def when(condition, action):
@@ -72,10 +73,10 @@
 
 
 def kernel(plan, tokens, gain, wq, wk, wv, wo, out, gathered,
-           tok, gw, nrm, part, recv, fin, ret, heads, nv, br, br_acc,
+           tok, gw, nrm, part, recv, fin, ret, heads, nv, nv_late, br, br_acc,
            w_rx, w_in, w_out, w_sib, w_loc, n_rx, n_in, n_out, n_sib,
            x_rx, x_tx, x_loc, g_rx, g_tx, r_rx, r_tx, ret_rx, ret_tx,
-           h_rx, h_tx, b_rx, b_tx, b_loc, nv_sem):
+           h_rx, h_tx, b_rx, b_tx, b_loc, nv_sem, nl_sem):
     G, S, C = plan.group, plan.stops, plan.chunks
     cw, depth, width, count = plan.chunk, plan.depth, plan.width, plan.count
     length, lw, fold, turns = plan.length, plan.local_width, plan.fold, plan.turns
@@ -89,7 +90,6 @@
     outward = (seq, (stop - toward) * CORES + core)
     sibling = (seq, stop * CORES + 1 - core)
     host = far >= 1 if fold else True
-    pending = []
 
     def remote(source, target, send, receive, device):
         return pltpu.make_async_remote_copy(
@@ -98,7 +98,6 @@
 
     def send(condition, make):
         when(condition, lambda: make().start())
-        pending.append((condition, make))
 
     def origin(i):
         return jnp.where(far >= i, stop - i * toward, stop + (i - far) * toward)
@@ -111,15 +110,15 @@
 
     def w_inward(j, o):
         b = block(j, o, core)
-        return remote(b, b, w_in.at[j, o], w_rx.at[j, o, core], inward)
+        return remote(b, b, w_in.at[0], w_rx.at[j, o], inward)
 
     def w_outward(j, o):
         b = block(j, o, core)
-        return remote(b, b, w_out.at[j, o], w_rx.at[j, o, core], outward)
+        return remote(b, b, w_out.at[0], w_rx.at[j, o], outward)
 
     def w_across(j, o):
         b = block(j, o, core)
-        return remote(b, b, w_sib.at[j, o], w_rx.at[j, o, core], sibling)
+        return remote(b, b, w_sib.at[0], w_rx.at[j, S], sibling)
 
     def w_arrive(i, j):
         with jax.named_scope(f"w{i}_{j}"):
@@ -130,7 +129,7 @@
 
         def take():
             b = block(j, o, core)
-            remote(b, b, w_sib.at[j, o], w_rx.at[j, o, core], sibling).wait_recv()
+            remote(b, b, w_sib.at[0], w_rx.at[j, o], sibling).wait_recv()
 
         when(host, take)
         if i <= S // 2 - 1:
@@ -148,10 +147,8 @@
 
     def w_other_core_body(j):
         def take():
-            for i in range(S):
-                o = stop if i == 0 else origin(i)
-                b = block(j, o, 1 - core)
-                remote(b, b, w_sib.at[j, o], w_rx.at[j, o, 1 - core], sibling).wait_recv()
+            b = gw.at[j, pl.ds(0, S * depth), :]
+            remote(b, b, w_sib.at[0], w_rx.at[j, S], sibling).wait_recv()
 
         when(host, take)
 
@@ -170,30 +167,43 @@
         r, cut = n_cut(pc)
         return gathered.at[o * CORES + c, r, cut]
 
-    def n_copy(o, pc, own, sems, device):
+    def n_copy(o, pc, own, sem, device):
         return remote(n_source(o, pc, own), n_target(o, core, pc),
-                      sems.at[o, pc], n_rx.at[o, core, pc], device)
+                      sem.at[0], n_rx.at[o, pc], device)
+
+    def n_across(i, pc):
+        o = stop if i == 0 else origin(i)
+        arrive = n_rx.at[S, pc] if i == S - 1 else n_rx.at[S + 1, i]
+        return remote(n_source(o, pc, i == 0), n_target(o, core, pc), n_sib.at[0], arrive, sibling)
+
+    def n_across_wait(i, pc=None):
+        if i == S - 1:
+            t = n_target(origin(i), 1 - core, pc)
+            remote(t, t, n_sib.at[0], n_rx.at[S, pc], sibling).wait_recv()
+        else:
+            t = gathered.at[0]
+            remote(t, t, n_sib.at[0], n_rx.at[S + 1, i], sibling).wait_recv()
 
     def n_own_in(condition, pc):
         send(condition, lambda: n_copy(stop, pc, True, n_in, inward))
 
-    def n_wait(o, c, pc):
-        t = n_target(o, c, pc)
-        remote(t, t, n_sib.at[o, pc], n_rx.at[o, c, pc], sibling).wait_recv()
+    def n_wait(o, pc):
+        t = n_target(o, core, pc)
+        remote(t, t, n_sib.at[0], n_rx.at[o, pc], sibling).wait_recv()
 
     def n_arrive(i, pc, who=True):
         o = origin(i)
 
         def take():
             with jax.named_scope(f"n{i}_{pc}"):
-                n_wait(o, core, pc)
+                n_wait(o, pc)
 
         when(who, take)
         if i <= S // 2 - 1:
             send(both_true(who, far >= i), lambda: n_copy(o, pc, False, n_in, inward))
         send(both_true(who, (far < i) & (far >= 1)),
              lambda: n_copy(o, pc, False, n_out, outward))
-        send(who, lambda: n_copy(o, pc, False, n_sib, sibling))
+        send(who, lambda: n_across(i, pc))
 
     barrier = pltpu.get_barrier_semaphore()
 
@@ -250,7 +260,7 @@
     def x_copy(k):
         d = flip(seq, k)
         return remote(tok.at[:, rows(d, width)], nrm.at[0, rows(seq, count), :],
-                      x_tx.at[k], x_rx.at[k], (d, fsdp))
+                      x_tx.at[0], x_rx.at[k], (d, fsdp))
 
     own_x = pltpu.make_async_copy(
         tok.at[:, rows(seq, width)], nrm.at[0, rows(seq, count), :], x_loc.at[1])
@@ -263,11 +273,11 @@
             own_x.wait()
         else:
             spot = nrm.at[0, rows(flip(seq, k), count), :]
-            remote(spot, spot, x_tx.at[k], x_rx.at[k], sibling).wait_recv()
+            remote(spot, spot, x_tx.at[0], x_rx.at[k], sibling).wait_recv()
 
     def g_copy(k):
         r = rows(flip(seq, k), count)
-        return remote(nrm.at[0, r, :], nrm.at[turns - 1, r, :], g_tx.at[k], g_rx.at[k], inward)
+        return remote(nrm.at[0, r, :], nrm.at[turns - 1, r, :], g_tx.at[0], g_rx.at[0], inward)
 
     guest = far < 1
     if fold:
@@ -279,13 +289,15 @@
         for pc in range(PIECES):
             n_own_in(guest, pc)
 
+    stages = len(orders(0, G))
+
     def project(j, low, high):
         with jax.named_scope(f"project_{j}"):
             project_body(j, low, high)
 
     def project_body(j, low, high):
         def step(i, carry):
-            t, k = i // G, G - 1 - i % G
+            t, k = high - 1 - i // G, G - 1 - i % G
             slot = j % SLOTS
             acc = jnp.dot(nrm[t], gw[j, :, rows(flip(seq, k), cw)], preferred_element_type=F32)
             for u in range(PAIR):
@@ -296,12 +308,26 @@
                 @pl.when((k // bit) % 2 == 1)
                 def _(u=u, bit=bit):
                     n = (k // (2 * bit)) * bit + k % bit
-                    remote(part.at[slot, t, u, k], recv.at[j, t, u, n], r_tx.at[j, t, u, k],
-                           r_rx.at[j, t, u, n], (flip(seq, bit), fsdp)).start()
+                    for q in range(1, stages + 1):
+                        if q < stages:
+                            mark = orders(u, G)[q]
+                            before = [b for b in orders(u, G)[1:q]]
+                        else:
+                            mark, before = 0, orders(u, G)[1:]
+                        hit = True
+                        for b in before:
+                            hit = both_true(hit, (k // b) % 2 == 0)
+                        if mark:
+                            hit = both_true(hit, (k // mark) % 2 == 1)
+
+                        @pl.when(hit)
+                        def _(q=q):
+                            remote(part.at[slot, t, u, k], recv.at[j, t, u, n], r_tx.at[j],
+                                   r_rx.at[j, t, q - 1], (flip(seq, bit), fsdp)).start()
 
             return carry
 
-        lax.fori_loop(low * G, high * G, step, 0)
+        lax.fori_loop(0, (high - low) * G, step, 0)
 
     def alive(u, q):
         bits = orders(u, G)[:q]
@@ -310,17 +336,19 @@
     def landing(u, q, k):
         return sum(len(alive(u, p + 1)) for p in range(q)) + alive(u, q + 1).index(k)
 
-    stages = len(orders(0, G))
-
-    def r_wait(j, t, u, q, k):
-        n = landing(u, q, k)
-        spot = recv.at[j, t, u, n]
-        remote(spot, spot, r_tx.at[j, t, u, 1], r_rx.at[j, t, u, n], sibling).wait_recv()
+    def goes(u, k):
+        for q, b in enumerate(orders(u, G)):
+            if k & b:
+                return q
+        return stages
+
+    def r_wait(j, t, q):
+        units = sum(goes(0, k) for k in range(G) if goes(0, k) == q)
+        spot = recv.at[j, t, :, pl.ds(0, units)]
+        remote(spot, spot, r_tx.at[j], r_rx.at[j, t, q - 1], sibling).wait_recv()
 
     def total(j, t, u, upto, k, store):
         tile = 128
-        for q in range(upto):
-            r_wait(j, t, u, q, k)
 
         def step(i, carry):
             r = rows(i, tile)
@@ -338,6 +366,7 @@
 
     def stage_body(j, t):
         for q in range(1, stages):
+            r_wait(j, t, q)
             for u in range(PAIR):
                 bit = orders(u, G)[q]
                 for k in reversed(alive(u, q)):
@@ -347,18 +376,18 @@
 
                         total(j, t, u, q, k, put)
                         n = landing(u, q, k ^ bit)
-                        remote(part.at[j % SLOTS, t, u, k], recv.at[j, t, u, n],
-                               r_tx.at[j, t, u, k], r_rx.at[j, t, u, n],
-                               (flip(seq, bit), fsdp)).start()
+                        remote(part.at[j % SLOTS, t, u, k], recv.at[j, t, u, n], r_tx.at[j],
+                               r_rx.at[j, t, goes(u, k ^ bit) - 1], (flip(seq, bit), fsdp)).start()
 
     def ret_copy(j):
-        return remote(ret.at[j], fin.at[j], ret_tx.at[j], ret_rx.at[j], outward)
+        return remote(ret.at[j], fin.at[j], ret_tx.at[0], ret_rx.at[j], outward)
 
     def settle(j, t):
         with jax.named_scope(f"settle_{j}_{t}"):
             settle_body(j, t)
 
     def settle_body(j, t):
+        r_wait(j, t, stages)
         for u in range(PAIR):
             def put(r, value, u=u):
                 if t:
@@ -372,19 +401,14 @@
 
     def returned(j):
         if fold:
-            pending.append((host, lambda: ret_copy(j)))
-
             @pl.when(guest)
             def _():
                 with jax.named_scope(f"returned_{j}"):
-                    remote(fin.at[j], fin.at[j], ret_tx.at[j], ret_rx.at[j], sibling).wait_recv()
+                    remote(fin.at[j], fin.at[j], ret_tx.at[0], ret_rx.at[j], sibling).wait_recv()
 
     def sent(j):
-        for t in range(turns):
-            for u in range(PAIR):
-                for k in range(1, G):
-                    p = part.at[j % SLOTS, t, u, k]
-                    remote(p, p, r_tx.at[j, t, u, k], r_rx.at[j, t, u, 0], sibling).wait_send()
+        p = part.at[j % SLOTS, :, :, pl.ds(0, G - 1)]
+        remote(p, p, r_tx.at[j], r_rx.at[j, 0, 0], sibling).wait_send()
 
     relayed = G == 4
     near = [1, 2] if relayed else list(range(1, G))
@@ -397,18 +421,17 @@
 
     def h_copy(j, k):
         spot = h_spot(seq, j)
-        return remote(spot, spot, h_tx.at[j, k], h_rx.at[j, k], (flip(seq, k), fsdp))
+        return remote(spot, spot, h_tx.at[0], h_rx.at[j, 0], (flip(seq, k), fsdp))
 
     def h_relay(j, u):
-        came, goes = orders(u, G)[:2]
+        came, then = orders(u, G)[:2]
         half = h_half(flip(seq, came), j, u)
-        return remote(half, half, h_tx.at[j, G + u], h_rx.at[j, G + u], (flip(seq, goes), fsdp))
+        return remote(half, half, h_tx.at[0], h_rx.at[j, 1], (flip(seq, then), fsdp))
 
     def h_wait(j):
         with jax.named_scope(f"hwait_{j}"):
-            for k in near:
-                spot = h_spot(flip(seq, k), j)
-                remote(spot, spot, h_tx.at[j, k], h_rx.at[j, k], sibling).wait_recv()
+            spot = heads.at[:, pl.ds(0, len(near) * cw)]
+            remote(spot, spot, h_tx.at[0], h_rx.at[j, 0], sibling).wait_recv()
 
     def relay(j):
         h_wait(j)
@@ -419,14 +442,11 @@
     def h_last(j):
         if relayed:
             with jax.named_scope(f"hlast_{j}"):
-                for u in range(PAIR):
-                    half = h_half(flip(seq, G - 1), j, u)
-                    remote(half, half, h_tx.at[j, G + u], h_rx.at[j, G + u], sibling).wait_recv()
+                spot = h_spot(seq, j)
+                remote(spot, spot, h_tx.at[0], h_rx.at[j, 1], sibling).wait_recv()
 
     def attend(j, condition=True):
         when(condition, lambda: mix(j))
-        for k in near:
-            pending.append((condition, lambda k=k: h_copy(j, k)))
 
     def mix(j):
         with jax.named_scope(f"attend_{j}"):
@@ -465,18 +485,14 @@
             return out.at[b]
         return out.at[:, rows(b * plan.parts + h, pw)]
 
-    def n_spot(h, c, r):
-        if plan.flat:
-            return nv.at[h, 0, r, pl.ds(c * pw, pw)]
-        return nv.at[h, c, r, :]
-
-    def n_load(o, own, h, r):
+    def n_load(o, own, h, r, spot, sems):
         copies = []
         for n in range(CORES):
             c = core if n == 0 else 1 - core
             cut = pl.ds(h * pw, pw)
             source = wo.at[r, cut] if own and n == 0 else gathered.at[o * CORES + c, r, cut]
-            copies.append(pltpu.make_async_copy(source, n_spot(h, n, r), nv_sem.at[h, n]))
+            where = spot.at[0, :, pl.ds(n * pw, pw)] if plan.flat else spot.at[n]
+            copies.append(pltpu.make_async_copy(source, where, sems.at[h, n]))
         return copies
 
     def br_spot(o, h, n, r):
@@ -490,46 +506,98 @@
             for k in range(1, G):
                 d = flip(seq, k)
                 remote(br_spot(o, h, n, rows(d, count)), target(o * CORES + c, h),
-                       b_tx.at[k], b_rx.at[k], (d, fsdp)).start()
+                       b_tx.at[0], b_rx.at[0], (d, fsdp)).start()
             pltpu.make_async_copy(br_spot(o, h, n, rows(seq, count)), target(o * CORES + c, h),
                                   b_loc.at[0]).start()
 
     tile = 256
-    whole = pl.ds(0, plan.rows_out)
-
-    def branch(o, own):
-        with jax.named_scope("branch"):
-            branch_body(o, own)
-
-    def branch_body(o, own):
-        copies = [n_load(o, own, h, whole) for h in range(plan.parts)]
-        for pair in copies:
-            for copy in pair:
-                copy.start()
+    ahead, late = (C - 2) * cw, cw
+
+    def strips(i, o, own, start, size, place, sems):
         for h in range(plan.parts):
-            for copy in copies[h]:
-                copy.wait()
-            for unit in range(plan.units):
-                def step(i, carry, h=h, unit=unit):
-                    r = rows(i, tile)
-                    acc = jnp.dot(heads[r, :], nv[h, unit], preferred_element_type=F32)
-                    br[o, h, unit, r, :] = acc.astype(BF16)
-                    return carry
-
-                lax.fori_loop(0, length // tile, step, 0)
-            br_send(o, h)
+            for d in range(G):
+                r = pl.ds(d * (C - 1) * cw + start, size)
+                for copy in n_load(o, own, h, r, place(h, d), sems):
+                    copy.start()
+
+    def strips_wait(place, sems):
+        for h in range(plan.parts):
+            for n in range(CORES):
+                spot = place(h)
+                where = spot.at[0, :, pl.ds(n * pw, pw)] if plan.flat else spot.at[n]
+                pltpu.make_async_copy(where, where, sems.at[h, n]).wait()
+
+    def early_load(i):
+        o = stop if i == 0 else origin(i)
+        strips(i, o, i == 0, ahead, late,
+               lambda h, d: nv_late.at[i % plan.kept, h, :, pl.ds(d * late, late), :], nl_sem)
+        if ahead:
+            strips(i, o, i == 0, 0, ahead,
+                   lambda h, d: nv.at[h, :, pl.ds(d * ahead, ahead), :], nv_sem)
+
+    def branch_early(i):
+        with jax.named_scope(f"early_{i}"):
+            strips_wait(lambda h: nv_late.at[i % plan.kept, h], nl_sem)
+            if ahead:
+                strips_wait(lambda h: nv.at[h, :, pl.ds(0, G * ahead), :], nv_sem)
+                for h in range(plan.parts):
+                    for unit in range(plan.units):
+                        def step(t, carry, h=h, unit=unit):
+                            r = rows(t, tile)
+                            acc = None
+                            for d in range(G):
+                                p = jnp.dot(heads[r, pl.ds(d * (C - 1) * cw, ahead)],
+                                            nv[h, unit, pl.ds(d * ahead, ahead), :],
+                                            preferred_element_type=F32)
+                                acc = p if acc is None else acc + p
+                            br_acc[i % plan.kept, h, unit, r, :] = acc
+                            return carry
+
+                        lax.fori_loop(0, length // tile, step, 0)
+
+    def branch(i):
+        with jax.named_scope(f"branch_{i}"):
+            o = stop if i == 0 else origin(i)
+            for h in range(plan.parts):
+                for unit in range(plan.units):
+                    def step(t, carry, h=h, unit=unit):
+                        r = rows(t, tile)
+                        acc = br_acc[i % plan.kept, h, unit, r, :] if ahead else None
+                        for d in range(G):
+                            p = jnp.dot(heads[r, pl.ds(d * (C - 1) * cw + ahead, late)],
+                                        nv_late[i % plan.kept, h, unit, pl.ds(d * late, late), :],
+                                        preferred_element_type=F32)
+                            acc = p if acc is None else acc + p
+                        br[o, h, unit, r, :] = acc.astype(BF16)
+                        return carry
+
+                    lax.fori_loop(0, length // tile, step, 0)
+                br_send(o, h)
 
     def branch_last(i):
         o = origin(i)
+
+        def loads(pc):
+            cut = pl.ds(pc % per_part * piece, piece)
+            h = pc // per_part
+            return n_load(o, False, h, cut, nv.at[h, :, cut, :], nl_sem if pc % 2 else nv_sem)
+
+        begun = 0
+
+        def begin(last):
+            nonlocal begun
+            while begun <= min(last, PIECES - 1):
+                polls(i, begun, begun + 1)
+                with jax.named_scope(f"nsib_{i}_{begun}"):
+                    n_across_wait(i, begun)
+                for copy in loads(begun):
+                    copy.start()
+                begun += 1
+
         for pc in range(PIECES):
-            polls(i, pc, pc + 2)
-            with jax.named_scope(f"nsib_{i}_{pc}"):
-                n_wait(o, 1 - core, pc)
+            begin(pc + 1 if pc < PIECES - 2 else pc)
             h, q = pc // per_part, pc % per_part
-            copies = n_load(o, False, h, pl.ds(q * piece, piece))
-            for copy in copies:
-                copy.start()
-            for copy in copies:
+            for copy in loads(pc):
                 copy.wait()
             for unit in range(plan.units):
                 def step(i, carry, h=h, q=q, unit=unit):
@@ -537,9 +605,9 @@
                     cut = pl.ds(q * piece, piece)
                     acc = jnp.dot(heads[r, cut], nv[h, unit, cut, :], preferred_element_type=F32)
                     if q:
-                        acc = acc + br_acc[unit, r, :]
+                        acc = acc + br_acc[plan.kept, h, unit, r, :]
                     if q < per_part - 1:
-                        br_acc[unit, r, :] = acc
+                        br_acc[plan.kept, h, unit, r, :] = acc
                     else:
                         br[o, h, unit, r, :] = acc.astype(BF16)
                     return carry
@@ -549,7 +617,7 @@
                 br_send(o, h)
 
     def both(action):
-        for t in range(turns):
+        for t in reversed(range(turns)):
             action(t)
 
     early = min(2, C)
@@ -576,7 +644,7 @@
         when(host, lambda j=j: project(j, 0, 1))
         if j == 0:
             for pc in range(PIECES):
-                send(True, lambda pc=pc: n_copy(stop, pc, True, n_sib, sibling))
+                send(True, lambda pc=pc: n_across(0, pc))
 
     def own_early():
         for j in range(early):
@@ -588,16 +656,12 @@
 
     def guests_early():
         with jax.named_scope("gwait"):
-            for k in range(G):
-                r = nrm.at[1, rows(flip(seq, k), count), :]
-                remote(r, r, g_tx.at[k], g_rx.at[k], sibling).wait_recv()
+            r = nrm.at[1]
+            remote(r, r, g_tx.at[0], g_rx.at[0], sibling).wait_recv()
         for j in range(early):
             project(j, 1, 2)
 
     when(host, own_early)
-    for j in range(1, early):
-        for k in near:
-            pending.append((host, lambda j=j, k=k: h_copy(j, k)))
     taken = []
     relays = [j for j in range(1, C)]
 
@@ -614,10 +678,10 @@
                     n_arrive(i, pc, who)
 
     def gather(i):
-        polls(i, 0, 8)
+        if i:
+            polls(i, 0, 8)
         with jax.named_scope(f"nsib_{i}"):
-            for pc in range(PIECES):
-                n_wait(origin(i), 1 - core, pc)
+            n_across_wait(i)
 
     def relay_to(j):
         while relays and relays[0] <= j:
@@ -626,82 +690,116 @@
     def close(j):
         when(host, lambda: both(lambda t: settle(j, t)))
         returned(j)
+
+    later = max(1, C - 1 - early)
+    step_pieces = (PIECES - FILL) // later
+    sent_in = FILL
+
+    def fill(count):
+        nonlocal sent_in
+        for pc in range(sent_in, min(PIECES, sent_in + count)):
+            n_own_in(host, pc)
+        sent_in = min(PIECES, sent_in + count)
 
     def forward(j):
         if early <= j < C:
             w_arrive(1, j)
             if j + 1 < C:
+                fill(step_pieces)
                 w_own_in(host, j + 1)
+
+    def attend_to(j):
+        close(j)
+        attend(j)
 
     polls(2, 0, 2, "host")
     if fold:
         when(host, guests_early)
-    polls(2, 2, 5, "host")
+    polls(2, 2, 4, "host")
     forward(early)
     if fold:
         when(host, lambda: both_early(stage))
-    polls(2, 5, FILL, "host")
-    if fold:
         when(host, lambda: both_early(settle))
-    for j in range(early + 1, C):
-        forward(j)
-    for pc in range(FILL, PIECES):
-        n_own_in(host, pc)
+    forward(early + 1)
     if fold:
         polls(1, 0, 8, "guest")
-        polls(2, 0, FILL, "guest")
+        polls(2, 0, 4, "guest")
         for e in range(early):
             returned(e)
         for e in range(1, early):
             attend(e, guest)
-    waiting = None
     for j in range(early, C):
         take_chunk(j)
+        last = j == C - 1
+        if last:
+            polls(1, 6, 8, "host")
+            relay_to(j - 1)
         if j >= SLOTS:
             when(host, lambda j=j: sent(j - SLOTS))
-        when(host, lambda j=j: project(j, 0, turns))
-        if j == C - 1:
-            polls(1, 6, 8, "host")
-            polls(2, 6, 7, "host")
-        if waiting is not None:
-            close(waiting)
+        if last and fold:
+            when(host, lambda j=j: project(j, 1, 2))
+            polls(3, 0, 1, "host")
+            when(host, lambda j=j: project(j, 0, 1))
+        else:
+            when(host, lambda j=j: project(j, 0, turns))
+        if last:
+            break
         relay_to(j - 2)
         when(host, lambda j=j: both(lambda t: stage(j, t)))
-        if j == C - 1:
-            polls(2, 7, 8, "host")
-        if waiting is not None:
-            attend(waiting)
-        waiting = j
-        if j < C - 2:
-            close(j)
-            attend(j)
-            waiting = None
+        if j == early:
+            for e in range(early + 2, C):
+                forward(e)
+            fill(PIECES)
+            polls(2, 4, 6, "host")
         if j == C - 2:
+            polls(2, 6, 8, "host")
             polls(1, 0, 6, "host")
+        attend_to(j)
+        if j == early:
+            polls(2, 4, 6, "guest")
+    fill(PIECES)
+    relay_to(C - 2)
+    two_steps = fold and C > early
+    if two_steps:
+        polls(2, 0, 8, "guest")
+        gather(0)
+        early_load(0)
     polls(3, 0, 1, "host")
-    polls(2, 0, 8, "guest")
-    if waiting is not None:
-        close(waiting)
-        attend(waiting)
-    polls(3, 1, 2, "host")
-    relay_to(C - 2)
-    polls(3, 2, 3, "host")
+    for j in range(1, C - 1):
+        h_last(j)
+    if two_steps:
+        branch_early(0)
+        gather(1)
+        early_load(1)
+        polls(3, 1, 2, "host")
+    if C > early:
+        when(host, lambda: both(lambda t: stage(C - 1, t)))
+    if two_steps:
+        branch_early(1)
+        gather(2)
+        early_load(2)
+        polls(3, 2, 3, "host")
+    if C > early:
+        attend_to(C - 1)
+    if two_steps:
+        polls(3, 3, 4, "host")
+        branch_early(2)
+        polls(3, 4, 5, "host")
+        polls(3, 0, 3, "guest")
     relay_to(C - 1)
-    polls(3, 3, 4, "host")
-    polls(3, 0, 2, "guest")
-    for j in range(1, C):
-        h_last(j)
-    for pc in range(PIECES):
-        n_wait(stop, 1 - core, pc)
-    branch(stop, True)
-    polls(3, 4, 5, "host")
-    polls(3, 2, 3, "guest")
-    for i in range(1, S - 1):
-        gather(i)
-        branch(origin(i), False)
-        polls(3, 4 + i, 5 + i, "host")
-        polls(3, 2 + i, 3 + i, "guest")
+    polls(3, 5, 6, "host")
+    polls(3, 3, 4, "guest")
+    h_last(C - 1)
+    polls(3, 6, 7, "host")
+    polls(3, 4, 5, "guest")
+    for i in range(S - 1):
+        if not two_steps:
+            gather(i)
+            early_load(i)
+            branch_early(i)
+        branch(i)
     polls(3, 0, 8, "host")
+    polls(3, 5, 6, "guest")
     if S > 1:
         branch_last(S - 1)
 
@@ -709,14 +807,47 @@
         span = plan.devices * plan.cols_out
         return out.at[:, rows(side, span)] if plan.flat else out.at[rows(side, plan.devices)]
 
+    def left(sem, count, spot):
+        def wait():
+            t = spot(count)
+            remote(t, t, sem.at[0], r_rx.at[0, 0, 0], sibling).wait_send()
+
+        return wait
+
     with jax.named_scope("sends"):
-        for condition, make in pending:
-            when(condition, lambda make=make: make().wait_send())
+        def w_spot(n):
+            return gw.at[:, pl.ds(0, n * depth), :]
+
+        def n_spot(n):
+            return gathered.at[pl.ds(0, n)]
+
+        for v in range(S // 2):
+            there = far == v
+            pl.when(there)(left(n_in, 1 + v, n_spot))
+            pl.when(there)(left(w_in, 1 + v, w_spot))
+            if v:
+                pl.when(there)(left(n_out, S - v, n_spot))
+                if not fold:
+                    pl.when(there)(left(w_out, S - v, w_spot))
+        left(n_sib, S, n_spot)()
+        when(host, left(w_sib, S, w_spot))
+        left(x_tx, G - 1, lambda n: tok.at[:, pl.ds(0, n * width)])()
+        left(h_tx, G - 1, lambda n: heads.at[:, pl.ds(0, n * lw)])()
+        if fold:
+            pl.when(guest)(left(g_tx, 0, lambda n: nrm.at[0]))
+            pl.when(host)(left(ret_tx, 0, lambda n: ret))
         when(host, lambda: [sent(j) for j in range(max(0, C - SLOTS), C)])
+
+    def others(first, n):
+        if plan.flat:
+            return out.at[:, pl.ds(first, n * plan.devices * plan.cols_out)]
+        return out.at[pl.ds(first, n * plan.devices)]
+
     with jax.named_scope("bwait"):
-        for k in range(1, G):
-            remote(all_of(seq), all_of(flip(seq, k)), b_tx.at[k], b_rx.at[k], sibling).wait()
-        pltpu.make_async_copy(all_of(seq), all_of(seq), b_loc.at[0]).wait()
+        spot = others(0, G - 1)
+        remote(spot, spot, b_tx.at[0], b_rx.at[0], sibling).wait()
+        spot = others(0, 1)
+        pltpu.make_async_copy(spot, spot, b_loc.at[0]).wait()
 
 
 def body(tokens, norm_gain, w_query, key_weight, value_weight, w_out):
@@ -731,7 +862,7 @@
         out_shape = (plan.count, plan.features)
     else:
         out_shape = (G * devices, plan.count, plan.cols_out)
-    outward = (1, 1) if plan.fold else (C, S)
+    stages = len(orders(0, G))
     branches, _ = pl.pallas_call(
         functools.partial(kernel, plan),
         out_shape=(
@@ -750,13 +881,14 @@
             pltpu.VMEM((C if plan.fold else 1, length, cw), BF16),
             pltpu.VMEM((length, plan.rows_out), BF16),
             pltpu.VMEM((plan.parts, plan.units, plan.rows_out, unit_cols), BF16),
+            pltpu.VMEM((plan.kept, plan.parts, plan.units, G * cw, unit_cols), BF16),
             pltpu.VMEM((S, plan.parts, plan.units, length, unit_cols), BF16),
-            pltpu.VMEM((plan.units, length, unit_cols), F32),
-            dma((C, S, CORES)), dma((C, S)), dma(outward), dma((C, S)), dma((C,)),
-            dma((S, CORES, PIECES)), dma((S, PIECES)), dma((S, PIECES)), dma((S, PIECES)),
-            dma((G,)), dma((G,)), dma((2,)), dma((G,)), dma((G,)),
-            dma((C, T, PAIR, G)), dma((C, T, PAIR, G)), dma((C,)), dma((C,)),
-            dma((C, G + PAIR)), dma((C, G + PAIR)), dma((G,)), dma((G,)), dma((1,)), dma((plan.parts, CORES)),
+            pltpu.VMEM((plan.kept + 1, plan.parts, plan.units, length, unit_cols), F32),
+            dma((C, S + 1)), dma((1,)), dma((1,)), dma((1,)), dma((C,)),
+            dma((S + 2, max(PIECES, S))), dma((1,)), dma((1,)), dma((1,)),
+            dma((G,)), dma((1,)), dma((2,)), dma((1,)), dma((1,)),
+            dma((C, T, stages)), dma((C,)), dma((C,)), dma((1,)),
+            dma((C, 2)), dma((1,)), dma((1,)), dma((1,)), dma((1,)), dma((plan.parts, CORES)), dma((plan.parts, CORES)),
         ],
         compiler_params=pltpu.CompilerParams(
             collective_id=0, has_side_effects=True, vmem_limit_bytes=67043328),

time: 249 us -> 244 us (0.980)
  Pallas kernels: 244 us -> 239 us
    pallas_call x1, Pallas kernels: 244 us -> 239 us  [body(): pl.pallas_call(functools.partial(kernel, plan), out_shape=(jax.ShapeDtype...]
where the time goes in v2:
time: 244 us; the launch traced here: 243 us
  Pallas kernels  239 us (98%)
  other arithmetic  4.76 us (2%)
    pallas_call x1, Pallas kernels, body(): pl.pallas_call(functools.partial(kernel, plan), out_shape=(jax.ShapeDtype...  239 us

profile of v2, /device:TPU:0, one launch (start us, length us, event | category | flops | bytes accessed | tf_op | source)
XLA Modules:
  0.0 243.5 jit_solution(1786302623335361126)
XLA Ops:
  0.0 238.7 %shard_map.64 = (bf16[128,8192]{1,0:T(8,128)(2,1)}, bf16[8,4096,256]{2,1,0:T(8,128)(2,1)}) custom-call(bf16[128,8192]{1,0:T(8,128)(2,1)} %bitcast.5, f32[1,8192]{1,0:T(1,128)} %bitcast.6, bf16[256,4096]{1,0:T(8,128)(2,1)} %wq.1, bf16[256,512]{1,0:T(8,128)(2,1)} %wk.1, bf16[256,512]{1,0:T(8,128)(2,1)} %wv.1, bf16[4096,256]{1,0:T(8,128)(2,1)} %wo.1), custom_call_target="tpu_custom_call" | custom-call | tf_op jit(solution)/shard_map/pallas_call | solution.py:866
  238.7 4.8 %convert_add_fusion = f32[1,128,8192]{2,1,0:T(8,128)} fusion(bf16[1,128,8192]{2,1,0:T(8,128)(2,1)} %param.6, bf16[128,8192]{1,0:T(8,128)(2,1)} %get-tuple-element.6), kind=kLoop, calls=%fused_computation | loop fusion | flops 3145728 | bytes 8388608 | tf_op jit(solution)/shard_map/add | solution.py:898

commit v3 on v2

--- a/solution.py
+++ b/solution.py
@@ -12,7 +12,8 @@
 PAIR = 2
 SLOTS = 2
 PIECES = 8
-FILL = 4
+FILL = 5
+TAIL = 1
 MESH = pl.DeviceIdType.MESH
 F32, BF16 = jnp.float32, jnp.bfloat16
 
@@ -21,8 +22,6 @@
     def __init__(self, group, devices, tokens, w_query, key_weight, w_out):
         self.group, self.devices = group, devices
         self.stops = devices // CORES
-        self.fold = self.stops == 4
-        self.turns = 2 if self.fold else 1
         self.count, self.features = tokens.shape
         self.width = self.features // group
         self.depth = self.width // devices
@@ -37,6 +36,8 @@
         self.flat = self.cols_out % HEAD == 0
         self.parts = self.cols_out // HEAD if self.flat else 1
         self.part_cols = self.cols_out // self.parts
+        self.fold = self.stops == 4 and self.flat
+        self.turns = 2 if self.fold else 1
         self.part_rows = PIECES // self.parts
         self.units = 1 if self.flat else CORES
         self.kept = self.stops - 1 if self.fold else 1
@@ -73,7 +74,7 @@
 
 
 def kernel(plan, tokens, gain, wq, wk, wv, wo, out, gathered,
-           tok, gw, nrm, part, recv, fin, ret, heads, nv, nv_late, br, br_acc,
+           tok, gw, nrm, part, recv, fin, ret, heads, nv, nv_late, nl, br, br_acc,
            w_rx, w_in, w_out, w_sib, w_loc, n_rx, n_in, n_out, n_sib,
            x_rx, x_tx, x_loc, g_rx, g_tx, r_rx, r_tx, ret_rx, ret_tx,
            h_rx, h_tx, b_rx, b_tx, b_loc, nv_sem, nl_sem):
@@ -159,26 +160,30 @@
     def n_cut(pc):
         return pl.ds(pc % per_part * piece, piece), pl.ds(pc // per_part * pw, pw)
 
-    def n_source(o, pc, own):
-        r, c = n_cut(pc)
-        return wo.at[r, c] if own else gathered.at[o * CORES + core, r, c]
-
-    def n_target(o, c, pc):
+    def n_place(o, c, pc, last):
         r, cut = n_cut(pc)
+        if last and fold:
+            return nl.at[pc // per_part, r, rows(c, pw)]
         return gathered.at[o * CORES + c, r, cut]
 
-    def n_copy(o, pc, own, sem, device):
-        return remote(n_source(o, pc, own), n_target(o, core, pc),
+    def n_source(o, pc, own, last):
+        r, cut = n_cut(pc)
+        return wo.at[r, cut] if own else n_place(o, core, pc, last)
+
+    def n_copy(o, pc, own, sem, device, last=False, lands_last=False):
+        return remote(n_source(o, pc, own, last), n_place(o, core, pc, lands_last),
                       sem.at[0], n_rx.at[o, pc], device)
 
     def n_across(i, pc):
         o = stop if i == 0 else origin(i)
-        arrive = n_rx.at[S, pc] if i == S - 1 else n_rx.at[S + 1, i]
-        return remote(n_source(o, pc, i == 0), n_target(o, core, pc), n_sib.at[0], arrive, sibling)
+        last = i == S - 1
+        arrive = n_rx.at[S, pc] if last else n_rx.at[S + 1, i]
+        return remote(n_source(o, pc, i == 0, last), n_place(o, core, pc, last),
+                      n_sib.at[0], arrive, sibling)
 
     def n_across_wait(i, pc=None):
         if i == S - 1:
-            t = n_target(origin(i), 1 - core, pc)
+            t = n_place(origin(i), 1 - core, pc, True)
             remote(t, t, n_sib.at[0], n_rx.at[S, pc], sibling).wait_recv()
         else:
             t = gathered.at[0]
@@ -187,8 +192,9 @@
     def n_own_in(condition, pc):
         send(condition, lambda: n_copy(stop, pc, True, n_in, inward))
 
-    def n_wait(o, pc):
-        t = n_target(o, core, pc)
+    def n_wait(i, pc):
+        o = origin(i)
+        t = n_place(o, core, pc, i == S - 1)
         remote(t, t, n_sib.at[0], n_rx.at[o, pc], sibling).wait_recv()
 
     def n_arrive(i, pc, who=True):
@@ -196,13 +202,13 @@
 
         def take():
             with jax.named_scope(f"n{i}_{pc}"):
-                n_wait(o, pc)
+                n_wait(i, pc)
 
         when(who, take)
         if i <= S // 2 - 1:
-            send(both_true(who, far >= i), lambda: n_copy(o, pc, False, n_in, inward))
+            send(both_true(who, far >= i), lambda: n_copy(o, pc, False, n_in, inward, False, True))
         send(both_true(who, (far < i) & (far >= 1)),
-             lambda: n_copy(o, pc, False, n_out, outward))
+             lambda: n_copy(o, pc, False, n_out, outward, i == S - 1, i == S - 1))
         send(who, lambda: n_across(i, pc))
 
     barrier = pltpu.get_barrier_semaphore()
@@ -500,9 +506,9 @@
             return br.at[o, h, 0, r, pl.ds(n * pw, pw)]
         return br.at[o, h, n, r, :]
 
-    def br_send(o, h):
+    def br_send(o, h, ordered=False):
         for n in range(CORES):
-            c = core if n == 0 else 1 - core
+            c = n if ordered else (core if n == 0 else 1 - core)
             for k in range(1, G):
                 d = flip(seq, k)
                 remote(br_spot(o, h, n, rows(d, count)), target(o * CORES + c, h),
@@ -590,20 +596,23 @@
                 polls(i, begun, begun + 1)
                 with jax.named_scope(f"nsib_{i}_{begun}"):
                     n_across_wait(i, begun)
-                for copy in loads(begun):
-                    copy.start()
+                if not fold:
+                    for copy in loads(begun):
+                        copy.start()
                 begun += 1
 
         for pc in range(PIECES):
             begin(pc + 1 if pc < PIECES - 2 else pc)
             h, q = pc // per_part, pc % per_part
-            for copy in loads(pc):
-                copy.wait()
+            if not fold:
+                for copy in loads(pc):
+                    copy.wait()
             for unit in range(plan.units):
                 def step(i, carry, h=h, q=q, unit=unit):
                     r = rows(i, tile)
                     cut = pl.ds(q * piece, piece)
-                    acc = jnp.dot(heads[r, cut], nv[h, unit, cut, :], preferred_element_type=F32)
+                    w = nl[h, cut, :] if fold else nv[h, unit, cut, :]
+                    acc = jnp.dot(heads[r, cut], w, preferred_element_type=F32)
                     if q:
                         acc = acc + br_acc[plan.kept, h, unit, r, :]
                     if q < per_part - 1:
@@ -614,7 +623,7 @@
 
                 lax.fori_loop(0, length // tile, step, 0)
             if q == per_part - 1:
-                br_send(o, h)
+                br_send(o, h, fold)
 
     def both(action):
         for t in reversed(range(turns)):
@@ -691,8 +700,6 @@
         when(host, lambda: both(lambda t: settle(j, t)))
         returned(j)
 
-    later = max(1, C - 1 - early)
-    step_pieces = (PIECES - FILL) // later
     sent_in = FILL
 
     def fill(count):
@@ -705,7 +712,7 @@
         if early <= j < C:
             w_arrive(1, j)
             if j + 1 < C:
-                fill(step_pieces)
+                fill((PIECES - TAIL - sent_in) // (C - 1 - j))
                 w_own_in(host, j + 1)
 
     def attend_to(j):
@@ -734,11 +741,15 @@
         if last:
             polls(1, 6, 8, "host")
             relay_to(j - 1)
+            if fold:
+                polls(2, 0, 8 - TAIL, "guest")
+                gather(0)
+                early_load(0)
         if j >= SLOTS:
             when(host, lambda j=j: sent(j - SLOTS))
         if last and fold:
             when(host, lambda j=j: project(j, 1, 2))
-            polls(3, 0, 1, "host")
+            polls(2, 8 - TAIL, 8, "host")
             when(host, lambda j=j: project(j, 0, 1))
         else:
             when(host, lambda j=j: project(j, 0, turns))
@@ -752,7 +763,7 @@
             fill(PIECES)
             polls(2, 4, 6, "host")
         if j == C - 2:
-            polls(2, 6, 8, "host")
+            polls(2, 6, 8 - TAIL, "host")
             polls(1, 0, 6, "host")
         attend_to(j)
         if j == early:
@@ -760,10 +771,6 @@
     fill(PIECES)
     relay_to(C - 2)
     two_steps = fold and C > early
-    if two_steps:
-        polls(2, 0, 8, "guest")
-        gather(0)
-        early_load(0)
     polls(3, 0, 1, "host")
     for j in range(1, C - 1):
         h_last(j)
@@ -771,16 +778,17 @@
         branch_early(0)
         gather(1)
         early_load(1)
-        polls(3, 1, 2, "host")
     if C > early:
         when(host, lambda: both(lambda t: stage(C - 1, t)))
     if two_steps:
+        polls(3, 1, 2, "host")
         branch_early(1)
         gather(2)
         early_load(2)
+    if C > early:
+        close(C - 1)
         polls(3, 2, 3, "host")
-    if C > early:
-        attend_to(C - 1)
+        attend(C - 1)
     if two_steps:
         polls(3, 3, 4, "host")
         branch_early(2)
@@ -788,10 +796,8 @@
         polls(3, 0, 3, "guest")
     relay_to(C - 1)
     polls(3, 5, 6, "host")
-    polls(3, 3, 4, "guest")
     h_last(C - 1)
     polls(3, 6, 7, "host")
-    polls(3, 4, 5, "guest")
     for i in range(S - 1):
         if not two_steps:
             gather(i)
@@ -799,7 +805,7 @@
             branch_early(i)
         branch(i)
     polls(3, 0, 8, "host")
-    polls(3, 5, 6, "guest")
+    polls(3, 3, 6, "guest")
     if S > 1:
         branch_last(S - 1)
 
@@ -863,6 +869,7 @@
     else:
         out_shape = (G * devices, plan.count, plan.cols_out)
     stages = len(orders(0, G))
+    nv_rows = max(16, G * (C - 2) * cw) if plan.fold else plan.rows_out
     branches, _ = pl.pallas_call(
         functools.partial(kernel, plan),
         out_shape=(
@@ -880,8 +887,9 @@
             pltpu.VMEM((C, length, cw), BF16),
             pltpu.VMEM((C if plan.fold else 1, length, cw), BF16),
             pltpu.VMEM((length, plan.rows_out), BF16),
-            pltpu.VMEM((plan.parts, plan.units, plan.rows_out, unit_cols), BF16),
+            pltpu.VMEM((plan.parts, plan.units, nv_rows, unit_cols), BF16),
             pltpu.VMEM((plan.kept, plan.parts, plan.units, G * cw, unit_cols), BF16),
+            pltpu.VMEM((plan.parts, plan.rows_out if plan.fold else 16, unit_cols), BF16),
             pltpu.VMEM((S, plan.parts, plan.units, length, unit_cols), BF16),
             pltpu.VMEM((plan.kept + 1, plan.parts, plan.units, length, unit_cols), F32),
             dma((C, S + 1)), dma((1,)), dma((1,)), dma((1,)), dma((C,)),

time: 244 us -> 239 us (0.980)
  Pallas kernels: 239 us -> 234 us
    pallas_call x1, Pallas kernels: 239 us -> 234 us  [body(): pl.pallas_call(functools.partial(kernel, plan), out_shape=(jax.ShapeDtype...]
where the time goes in v3:
time: 239 us
  Pallas kernels  234 us (98%)
  other arithmetic  4.76 us (2%)
    pallas_call x1, Pallas kernels, body(): pl.pallas_call(functools.partial(kernel, plan), out_shape=(jax.ShapeDtype...  234 us

profile of v3, /device:TPU:0, one launch (start us, length us, event | category | flops | bytes accessed | tf_op | source)
XLA Modules:
  0.0 238.5 jit_solution(15368351443650492910)
XLA Ops:
  0.0 233.8 %shard_map.64 = (bf16[128,8192]{1,0:T(8,128)(2,1)}, bf16[8,4096,256]{2,1,0:T(8,128)(2,1)}) custom-call(bf16[128,8192]{1,0:T(8,128)(2,1)} %bitcast.5, f32[1,8192]{1,0:T(1,128)} %bitcast.6, bf16[256,4096]{1,0:T(8,128)(2,1)} %wq.1, bf16[256,512]{1,0:T(8,128)(2,1)} %wk.1, bf16[256,512]{1,0:T(8,128)(2,1)} %wv.1, bf16[4096,256]{1,0:T(8,128)(2,1)} %wo.1), custom_call_target="tpu_custom_call" | custom-call | tf_op jit(solution)/shard_map/pallas_call | solution.py:873
  233.8 4.8 %convert_add_fusion = f32[1,128,8192]{2,1,0:T(8,128)} fusion(bf16[1,128,8192]{2,1,0:T(8,128)(2,1)} %param.6, bf16[128,8192]{1,0:T(8,128)(2,1)} %get-tuple-element.6), kind=kLoop, calls=%fused_computation | loop fusion | flops 3145728 | bytes 8388608 | tf_op jit(solution)/shard_map/add | solution.py:906

commit v4 on v3

--- a/solution.py
+++ b/solution.py
@@ -750,7 +750,6 @@
         if last and fold:
             when(host, lambda j=j: project(j, 1, 2))
             polls(2, 8 - TAIL, 8, "host")
-            when(host, lambda j=j: project(j, 0, 1))
         else:
             when(host, lambda j=j: project(j, 0, turns))
         if last:
@@ -778,22 +777,26 @@
         branch_early(0)
         gather(1)
         early_load(1)
-    if C > early:
-        when(host, lambda: both(lambda t: stage(C - 1, t)))
-    if two_steps:
+        when(host, lambda: stage(C - 1, 1))
+        when(host, lambda: project(C - 1, 0, 1))
         polls(3, 1, 2, "host")
         branch_early(1)
         gather(2)
         early_load(2)
-    if C > early:
-        close(C - 1)
+        when(host, lambda: settle(C - 1, 1))
+        returned(C - 1)
+        attend(C - 1, guest)
         polls(3, 2, 3, "host")
-        attend(C - 1)
-    if two_steps:
+        branch_early(2)
+        when(host, lambda: stage(C - 1, 0))
         polls(3, 3, 4, "host")
-        branch_early(2)
+        when(host, lambda: settle(C - 1, 0))
+        attend(C - 1, host)
         polls(3, 4, 5, "host")
         polls(3, 0, 3, "guest")
+    elif C > early:
+        when(host, lambda: both(lambda t: stage(C - 1, t)))
+        attend_to(C - 1)
     relay_to(C - 1)
     polls(3, 5, 6, "host")
     h_last(C - 1)

time: 239 us -> 238 us (level)
  no operation moved by 1% of the time
where the time goes in v4:
time: 238 us
  Pallas kernels  233 us (98%)
  other arithmetic  4.76 us (2%)
    pallas_call x1, Pallas kernels, body(): pl.pallas_call(functools.partial(kernel, plan), out_shape=(jax.ShapeDtype...  233 us

profile of v4, /device:TPU:0, one launch (start us, length us, event | category | flops | bytes accessed | tf_op | source)
XLA Modules:
  0.0 238.2 jit_solution(13909151025780428048)
XLA Ops:
  0.0 233.4 %shard_map.64 = (bf16[128,8192]{1,0:T(8,128)(2,1)}, bf16[8,4096,256]{2,1,0:T(8,128)(2,1)}) custom-call(bf16[128,8192]{1,0:T(8,128)(2,1)} %bitcast.5, f32[1,8192]{1,0:T(1,128)} %bitcast.6, bf16[256,4096]{1,0:T(8,128)(2,1)} %wq.1, bf16[256,512]{1,0:T(8,128)(2,1)} %wk.1, bf16[256,512]{1,0:T(8,128)(2,1)} %wv.1, bf16[4096,256]{1,0:T(8,128)(2,1)} %wo.1), custom_call_target="tpu_custom_call" | custom-call | tf_op jit(solution)/shard_map/pallas_call | solution.py:876
  233.4 4.8 %convert_add_fusion = f32[1,128,8192]{2,1,0:T(8,128)} fusion(bf16[1,128,8192]{2,1,0:T(8,128)(2,1)} %param.6, bf16[128,8192]{1,0:T(8,128)(2,1)} %get-tuple-element.6), kind=kLoop, calls=%fused_computation | loop fusion | flops 3145728 | bytes 8388608 | tf_op jit(solution)/shard_map/add | solution.py:909
